TPU v7x, 1024 devices: a whole 8x8x8 slice. The times are simulated.
1024 devices in a mesh: sub: 16 (over z, core), wide: 64 (over y, x).
Axes of the slice: x: 8, y: 8, z: 8, core: 2. Of those that a mesh axis runs over, the one named last changes fastest.
Arguments:
- load_table: bfloat16 [16, 64, 16, 4, 128], P('sub', 'wide'), may hold values from -6 to 6
- load_column: int32 [64], replicated, may hold values from 0 to 15
- face_order: int32 [16, 64, 4], P('sub', 'wide'), may hold values from 0 to 3, each once within a row
- schur: bfloat16 [16, 64, 512, 512], P('sub', 'wide'), as said below
- neumann: bfloat16 [16, 64, 512, 512], P('sub', 'wide'), as said below
- coarse_basis: bfloat16 [16, 64, 4, 4, 128], P('sub', 'wide'), may hold values from -0.625 to 0.625
- corner_map: int32 [16, 64, 4], P('sub', 'wide'), may hold values from 0 to 1151, as said below
- coarse_inverse: float32 [1152, 1152], P('wide'), as said below
Outputs:
- solution: float32 [16, 64, 4, 64, 128], P('sub', 'wide')
Inputs may be any that keep to these rules, and one draw needn't show every extreme that they name: `corner_map`: each subdomain's 4 entries are distinct; subdomains that meet at a corner of the grid of subdomains give it the same number, and different corners get different numbers, so (17) * (65) of the 1152 numbers occur and the others belong to no corner. `coarse_inverse`: Symmetric. `schur`: Symmetric. `neumann`: Symmetric.
All inputs are finite; a program needn't handle non-finite values.
Results may differ from a plain program's by a relative error of at most 0.0014.
Values sent between devices are 32-bit elements; how exact they have to be, the bound alone decides.
No kernel may reach another device: no remote copies, remote signals or barrier semaphores. Data moves between devices by JAX's collectives and lax.ppermute only.
A program may use at most 32 MiB of HBM per device.

v0:
```python
import jax
import jax.numpy as jnp
from jax import lax
from jax.sharding import PartitionSpec as P

ITERS = 3


damping = 0.3


def padded_2(array, sides, width):
    edges = {}
    for axis, dim in sides:
        peers, length = (lax.axis_size(axis), array.shape[dim])
        up = [(i, (i + 1) % peers) for i in range(peers - 1)]
        last = lax.slice_in_dim(array, length - width, length, axis=dim)
        first = lax.slice_in_dim(array, 0, width, axis=dim)
        edges[dim] = (
            lax.ppermute(last, axis, up),
            lax.ppermute(first, axis, [(b, a) for a, b in up]),
        )
    done = []
    for _, dim in sides:
        low, high = edges[dim]
        around = [(width, width) if d in done else (0, 0) for d in range(array.ndim)]
        array = jnp.concatenate([jnp.pad(low, around), array, jnp.pad(high, around)], axis=dim)
        done.append(dim)
    return array


def split_up(array, dim, peers):
    lengths = array.shape
    tiles = array.reshape(*lengths[:dim], peers, lengths[dim] // peers, *lengths[dim + 1 :])
    return jnp.moveaxis(tiles, dim, 0)


def sum_at_owner(array, axis, dim):
    peers = lax.axis_size(axis)
    tiles = lax.all_to_all(split_up(array, dim, peers), axis, 0, 0, tiled=True)
    return jnp.sum(tiles, axis=0)


def copy_for_each(array, axis):
    peers = lax.axis_size(axis)
    return lax.all_to_all(
        jnp.broadcast_to(array[None], (peers, *array.shape)), axis, 0, 0, tiled=True
    )


def of_everyone(array, axis):
    everything = copy_for_each(array, axis)
    return jnp.sum(everything, axis=0)


def apply_local(vectors, operators, selector_half, selector_full):
    amount = vectors.shape[0]
    rhs_count = vectors.shape[3]
    face_width = vectors.shape[4]
    rounded = vectors.astype(jnp.bfloat16)
    blocked = jnp.einsum(
        "kcbf,kcfjn->kcjbn", selector_half, rounded, preferred_element_type=jnp.float32
    )
    blocked = blocked.astype(jnp.bfloat16).reshape(amount, 1, rhs_count, 4 * face_width)
    product = jnp.einsum("kcjm,kcmn->kcjn", blocked, operators, preferred_element_type=jnp.float32)
    product = product.reshape(amount, 1, rhs_count, 4, face_width)
    return jnp.einsum("kcbf,kcjbn->kcfjn", selector_full, product, precision=lax.Precision.HIGHEST)


def assemble(copies):
    padded = padded_2(copies, (("sub", 0), ("wide", 1)), 1)
    north_sum = copies[:, 0, 0] + padded[:-2, 1, 1]
    south_sum = copies[:, 0, 1] + padded[2:, 1, 0]
    west_sum = copies[:, 0, 2] + padded[1:-1, 0, 3]
    east_sum = copies[:, 0, 3] + padded[1:-1, 2, 2]
    return jnp.stack([north_sum, south_sum, west_sum, east_sum], axis=1)[:, None]


def coarse_solve(partial_value, coarse_inverse):
    owned_share = sum_at_owner(partial_value, "wide", 1)
    owned_share = of_everyone(owned_share, "sub")
    owned_term = jnp.dot(owned_share, coarse_inverse, precision=lax.Precision.HIGHEST)
    return lax.psum(owned_term, "wide")


def body(
    load_table, load_column, face_order, schur, neumann, coarse_basis, corner_map, coarse_inverse
):
    amount = schur.shape[0]
    pattern_count = load_table.shape[2]
    coarse_order = coarse_inverse.shape[1]
    selector_full = (face_order[..., :, None] == jnp.arange(4, dtype=jnp.int32)).astype(jnp.float32)
    selector_half = selector_full.astype(jnp.bfloat16)
    load_select = (load_column[:, None] == jnp.arange(pattern_count, dtype=jnp.int32)).astype(
        jnp.bfloat16
    )
    load_faces = jnp.einsum(
        "jl,kclfn->kcfjn", load_select, load_table, preferred_element_type=jnp.float32
    )
    row_ids = lax.axis_index("sub") * amount + jnp.arange(amount, dtype=jnp.int32)
    rows_total = amount * lax.axis_size("sub")
    column_index = lax.axis_index("wide") * jnp.ones((amount,), jnp.int32)
    cols_total = lax.axis_size("wide")
    half = jnp.float32(0.5)
    whole = jnp.float32(1.0)
    weights = jnp.stack(
        [
            jnp.where(row_ids > 0, half, whole),
            jnp.where(row_ids < rows_total - 1, half, whole),
            jnp.where(column_index > 0, half, whole),
            jnp.where(column_index < cols_total - 1, half, whole),
        ],
        axis=1,
    )[:, None, :, None, None]
    basis = coarse_basis.astype(jnp.float32)
    corner_marks = (corner_map[..., None] == jnp.arange(coarse_order, dtype=jnp.int32)).astype(
        jnp.float32
    )
    solution = jnp.zeros(load_faces.shape, jnp.float32)
    for iteration in range(ITERS):
        if iteration == 0:
            residual = assemble(load_faces)
        else:
            residual = assemble(
                load_faces - apply_local(solution, schur, selector_half, selector_full)
            )
        weighted = weights * residual
        restricted = jnp.einsum(
            "kcpfn,kcfjn->kcpj", basis, weighted, precision=lax.Precision.HIGHEST
        )
        partial_value = jnp.einsum(
            "kcpj,kcpg->jg", restricted, corner_marks, precision=lax.Precision.HIGHEST
        )
        neumann_part = apply_local(weighted, neumann, selector_half, selector_full)
        solved = coarse_solve(partial_value, coarse_inverse)
        picked = jnp.einsum("jg,kcpg->kcpj", solved, corner_marks, precision=lax.Precision.HIGHEST)
        correction = jnp.einsum("kcpj,kcpfn->kcfjn", picked, basis, precision=lax.Precision.HIGHEST)
        update = assemble(weights * (neumann_part + correction))
        solution = solution + damping * update
    return solution


def solution(mesh):
    in_specs = (
        P("sub", "wide", None, None, None),
        P(),
        P("sub", "wide", None),
        P("sub", "wide", None, None),
        P("sub", "wide", None, None),
        P("sub", "wide", None, None, None),
        P("sub", "wide", None),
        P("wide", None),
    )
    out_specs = P("sub", "wide", None, None, None)
    return jax.shard_map(body, mesh=mesh, in_specs=in_specs, out_specs=out_specs, check_vma=False)
```

profile of v0, /device:TPU:15, one launch (start us, length us, event | category | flops | bytes accessed | tf_op | source)
XLA Modules:
  0.0 743.5 jit_solution(4451776188804234635)
XLA Ops:
  6.5 0.7 copy-done.6
  7.2 0.9 convolution_bitcast_fusion.6
  8.2 3.1 collective-permute-start.2
  11.3 2.9 collective-permute-start.1
  14.1 2.2 collective-permute-start.3
  16.3 5.1 collective-permute-start
  21.5 1.8 collective-permute-done.3
  23.4 0.7 copy-done.3
  24.3 0.7 copy-done.4
  25.8 1.1 reshape.1341
  26.9 14.2 %all-to-all-start = ((f32[64,1,1152]{2,1,0:T(1,128)}), f32[64,1,1152]{2,1,0:T(1,128)S(1)}, u32[]{:S(2)}, u32[]{:S(2)}) async-start(f32[64,1,1152]{2,1,0:T(1,128)} %reshape.1341), calls=%async_computation | async-start | bytes 589824 | tf_op jit(solution)/shard_map/all_to_all | solution.py:40
  41.3 12.6 %all-to-all-done = f32[64,1,1152]{2,1,0:T(1,128)S(1)} async-done(((f32[64,1,1152]{2,1,0:T(1,128)}), f32[64,1,1152]{2,1,0:T(1,128)S(1)}, u32[]{:S(2)}, u32[]{:S(2)}) %all-to-all-start) | async-done | bytes 294944 | tf_op jit(solution)/shard_map/all_to_all | solution.py:40
  54.4 1.4 reduce
  56.1 0.8 reshape.1343
  56.9 16.1 %all-to-all-start.1 = ((f32[16,1,1152]{2,1,0:T(1,128)}), f32[16,1,1152]{2,1,0:T(1,128)S(1)}, u32[]{:S(2)}, u32[]{:S(2)}) async-start(f32[16,1,1152]{2,1,0:T(1,128)} %reshape.1343), calls=%async_computation.1 | async-start | bytes 147456 | tf_op jit(solution)/shard_map/all_to_all | solution.py:46
  74.0 6.9 all-to-all-done.1
  80.9 0.8 reduce.1
  81.9 1.2 fusion.116
  83.7 151.6 %all-reduce.4.cloned.1.call-done = f32[64,1152]{1,0:T(8,128)} async-done(((f32[64,1152]{1,0:T(8,128)}), f32[64,1152]{1,0:T(8,128)}) %all-reduce.4.cloned.1.call-update) | async-done | bytes 294928 | tf_op jit(solution)/shard_map/psum | solution.py:83
  235.3 1.2 convolution_bitcast_fusion.9
  236.8 4.3 collective-permute-start.6
  241.2 6.9 collective-permute-start.5
  248.0 3.4 collective-permute-start.4
  251.4 1.9 collective-permute-start.7
  253.6 6.6 collective-permute-done.7
  261.1 1.9 collective-permute-start.11
  263.0 2.1 collective-permute-start.9
  265.2 5.8 collective-permute-start.10
  270.9 3.6 collective-permute-start.8
  274.6 1.9 collective-permute-done.8
  278.0 22.0 %all_to_all.30 = f32[64,1,1152]{2,1,0:T(1,128)S(1)} all-to-all(f32[64,1,1152]{2,1,0:T(1,128)S(1)} %reshape.1345), channel_id=1, replica_groups=mesh['sub'=16,'wide'=64] {'wide'}, dimensions={0} | all-to-all | bytes 589824 | tf_op jit(solution)/shard_map/all_to_all | solution.py:40
  299.9 1.4 reduce.2
  301.7 0.8 reshape.1347
  302.4 9.9 %all-to-all-start.3 = ((f32[16,1,1152]{2,1,0:T(1,128)}), f32[16,1,1152]{2,1,0:T(1,128)S(1)}, u32[]{:S(2)}, u32[]{:S(2)}) async-start(f32[16,1,1152]{2,1,0:T(1,128)} %reshape.1347), calls=%async_computation.3 | async-start | bytes 147456 | tf_op jit(solution)/shard_map/all_to_all | solution.py:46
  312.9 7.4 all-to-all-done.3
  320.2 0.8 reduce.3
  321.2 1.2 fusion.119
  323.0 151.8 %all-reduce.6.cloned.1.call-done = f32[64,1152]{1,0:T(8,128)} async-done(((f32[64,1152]{1,0:T(8,128)}), f32[64,1152]{1,0:T(8,128)}) %all-reduce.6.cloned.1.call-update) | async-done | bytes 294928 | tf_op jit(solution)/shard_map/psum | solution.py:83
  474.9 1.2 convolution_bitcast_fusion.8
  476.4 4.3 collective-permute-start.14
  480.7 6.9 collective-permute-start.13
  487.6 3.4 collective-permute-start.12
  491.0 1.9 collective-permute-start.15
  492.9 6.8 collective-permute-done.15
  500.7 1.9 collective-permute-start.19
  502.6 2.1 collective-permute-start.17
  504.8 5.8 collective-permute-start.18
  510.5 3.6 collective-permute-start.16
  514.2 1.9 collective-permute-done.16
  517.5 22.0 %all_to_all.31 = f32[64,1,1152]{2,1,0:T(1,128)S(1)} all-to-all(f32[64,1,1152]{2,1,0:T(1,128)S(1)} %reshape.1349), channel_id=1, replica_groups=mesh['sub'=16,'wide'=64] {'wide'}, dimensions={0} | all-to-all | bytes 589824 | tf_op jit(solution)/shard_map/all_to_all | solution.py:40
  539.5 1.4 reduce.4
  541.2 0.8 reshape.1351
  542.0 9.9 %all-to-all-start.5 = ((f32[16,1,1152]{2,1,0:T(1,128)}), f32[16,1,1152]{2,1,0:T(1,128)S(1)}, u32[]{:S(2)}, u32[]{:S(2)}) async-start(f32[16,1,1152]{2,1,0:T(1,128)} %reshape.1351), calls=%async_computation.5 | async-start | bytes 147456 | tf_op jit(solution)/shard_map/all_to_all | solution.py:46
  552.3 7.5 %all-to-all-done.5 = f32[16,1,1152]{2,1,0:T(1,128)S(1)} async-done(((f32[16,1,1152]{2,1,0:T(1,128)}), f32[16,1,1152]{2,1,0:T(1,128)S(1)}, u32[]{:S(2)}, u32[]{:S(2)}) %all-to-all-start.5) | async-done | bytes 73760 | tf_op jit(solution)/shard_map/all_to_all | solution.py:46
  559.8 0.8 reduce.5
  560.8 1.2 fusion.122
  562.6 151.8 %all-reduce.8.cloned.1.call-done = f32[64,1152]{1,0:T(8,128)} async-done(((f32[64,1152]{1,0:T(8,128)}), f32[64,1152]{1,0:T(8,128)}) %all-reduce.8.cloned.1.call-update) | async-done | bytes 294928 | tf_op jit(solution)/shard_map/psum | solution.py:83
  714.4 1.2 convolution_bitcast_fusion.7
  716.0 2.6 collective-permute-start.23
  718.5 7.1 collective-permute-start.21
  725.7 5.0 collective-permute-start.22
  730.7 3.6 collective-permute-start.20
  734.3 1.9 collective-permute-done.20
  736.2 0.7 fusion.13
  (102 shorter events, 13.0 us)
Async XLA Ops:
  6.5 75.4 %copy-start = (f32[18,1152]{1,0:T(8,128)S(1)}, f32[18,1152]{1,0:T(8,128)}, u32[]{:S(2)}) copy-start(f32[18,1152]{1,0:T(8,128)} %param.15) | copy-start | bytes 248836
  6.5 0.7 copy-start.6
  8.2 13.4 %collective-permute-start.2 = (f32[1,1,4,64,128]{4,3,2,1,0:T(8,128)S(1)}, f32[1,1,4,64,128]{4,3,2,1,0:T(8,128)S(1)}, u32[]{:S(2)}, u32[]{:S(2)}) collective-permute-start(f32[1,1,4,64,128]{4,3,2,1,0:T(8,128)S(1)} %convolution_bitcast_fusion.6), channel_id=1, source_target_pairs={{0,1},{1,2},{2,3},{3,4},{4,5},{5,6},{6,7},{7,8},{8,9},{9,10},{10,1... | collective-permute-start | bytes 393224 | tf_op jit(solution)/shard_map/ppermute | solution.py:20
  11.3 10.2 %collective-permute-start.1 = (f32[1,1,4,64,128]{4,3,2,1,0:T(8,128)S(1)}, f32[1,1,4,64,128]{4,3,2,1,0:T(8,128)S(1)}, u32[]{:S(2)}, u32[]{:S(2)}) collective-permute-start(f32[1,1,4,64,128]{4,3,2,1,0:T(8,128)S(1)} %convolution_bitcast_fusion.6), channel_id=1, source_target_pairs={{64,0},{128,64},{192,128},{256,192},{320,256},{384,320},{448,384},... | collective-permute-start | bytes 393224 | tf_op jit(solution)/shard_map/ppermute | solution.py:21
  14.1 9.2 %collective-permute-start.3 = (f32[1,1,4,64,128]{4,3,2,1,0:T(8,128)S(1)}, f32[1,1,4,64,128]{4,3,2,1,0:T(8,128)S(1)}, u32[]{:S(2)}, u32[]{:S(2)}) collective-permute-start(f32[1,1,4,64,128]{4,3,2,1,0:T(8,128)S(1)} %convolution_bitcast_fusion.6), channel_id=1, source_target_pairs={{1,0},{2,1},{3,2},{4,3},{5,4},{6,5},{7,6},{8,7},{9,8},{10,9},{11,1... | collective-permute-start | bytes 393224 | tf_op jit(solution)/shard_map/ppermute | solution.py:21
  16.3 7.0 collective-permute-start
  23.4 0.7 copy-start.3
  24.3 0.7 copy-start.4
  26.9 14.2 %copy-start.1 = (bf16[1,1,512,512]{3,2,1,0:T(8,128)(2,1)S(1)}, bf16[1,1,512,512]{3,2,1,0:T(8,128)(2,1)}, u32[]{:S(2)}) copy-start(bf16[1,1,512,512]{3,2,1,0:T(8,128)(2,1)} %param.12) | copy-start | bytes 1572868
  26.9 27.0 %all-to-all-start = ((f32[64,1,1152]{2,1,0:T(1,128)}), f32[64,1,1152]{2,1,0:T(1,128)S(1)}, u32[]{:S(2)}, u32[]{:S(2)}) async-start(f32[64,1,1152]{2,1,0:T(1,128)} %reshape.1341), calls=%async_computation | async-start | bytes 589824 | tf_op jit(solution)/shard_map/all_to_all | solution.py:40
  56.9 24.0 %all-to-all-start.1 = ((f32[16,1,1152]{2,1,0:T(1,128)}), f32[16,1,1152]{2,1,0:T(1,128)S(1)}, u32[]{:S(2)}, u32[]{:S(2)}) async-start(f32[16,1,1152]{2,1,0:T(1,128)} %reshape.1343), calls=%async_computation.1 | async-start | bytes 147456 | tf_op jit(solution)/shard_map/all_to_all | solution.py:46
  73.0 162.3 %all-reduce.4.cloned.1.call-start = ((), (), s32[]{:S(2)}) async-start(), calls=%async_computation.6 | async-start | bytes 589824 | tf_op jit(solution)/shard_map/psum | solution.py:83
  73.1 0.7 copy-start.5
  83.4 170.0 %copy-start.2 = (bf16[1,1,512,512]{3,2,1,0:T(8,128)(2,1)S(1)}, bf16[1,1,512,512]{3,2,1,0:T(8,128)(2,1)}, u32[]{:S(2)}) copy-start(bf16[1,1,512,512]{3,2,1,0:T(8,128)(2,1)} %param.11) | copy-start | bytes 1572868
  236.8 16.7 %collective-permute-start.6 = (f32[1,1,4,64,128]{4,3,2,1,0:T(8,128)S(1)}, f32[1,1,4,64,128]{4,3,2,1,0:T(8,128)S(1)}, u32[]{:S(2)}, u32[]{:S(2)}) collective-permute-start(f32[1,1,4,64,128]{4,3,2,1,0:T(8,128)S(1)} %fusion.1), channel_id=1, source_target_pairs={{0,1},{1,2},{2,3},{3,4},{4,5},{5,6},{6,7},{7,8},{8,9},{9,10},{10,1... | collective-permute-start | bytes 393224 | tf_op jit(solution)/shard_map/ppermute | solution.py:20
  241.2 12.4 %collective-permute-start.5 = (f32[1,1,4,64,128]{4,3,2,1,0:T(8,128)S(1)}, f32[1,1,4,64,128]{4,3,2,1,0:T(8,128)S(1)}, u32[]{:S(2)}, u32[]{:S(2)}) collective-permute-start(f32[1,1,4,64,128]{4,3,2,1,0:T(8,128)S(1)} %fusion.1), channel_id=1, source_target_pairs={{64,0},{128,64},{192,128},{256,192},{320,256},{384,320},{448,384},... | collective-permute-start | bytes 393224 | tf_op jit(solution)/shard_map/ppermute | solution.py:21
  248.0 5.5 collective-permute-start.4
  251.4 8.8 %collective-permute-start.7 = (f32[1,1,4,64,128]{4,3,2,1,0:T(8,128)S(1)}, f32[1,1,4,64,128]{4,3,2,1,0:T(8,128)S(1)}, u32[]{:S(2)}, u32[]{:S(2)}) collective-permute-start(f32[1,1,4,64,128]{4,3,2,1,0:T(8,128)S(1)} %fusion.1), channel_id=1, source_target_pairs={{1,0},{2,1},{3,2},{4,3},{5,4},{6,5},{7,6},{8,7},{9,8},{10,9},{11,1... | collective-permute-start | bytes 393224 | tf_op jit(solution)/shard_map/ppermute | solution.py:21
  261.1 13.5 %collective-permute-start.11 = (f32[1,1,4,64,128]{4,3,2,1,0:T(8,128)S(1)}, f32[1,1,4,64,128]{4,3,2,1,0:T(8,128)S(1)}, u32[]{:S(2)}, u32[]{:S(2)}) collective-permute-start(f32[1,1,4,64,128]{4,3,2,1,0:T(8,128)S(1)} %bitcast_subtract_fusion.1), channel_id=1, source_target_pairs={{1,0},{2,1},{3,2},{4,3},{5,4},{6,5},{7,6},{8,7},{9,8},{10,9},{11,1... | collective-permute-start | bytes 393224 | tf_op jit(solution)/shard_map/ppermute | solution.py:21
  263.0 11.5 %collective-permute-start.9 = (f32[1,1,4,64,128]{4,3,2,1,0:T(8,128)S(1)}, f32[1,1,4,64,128]{4,3,2,1,0:T(8,128)S(1)}, u32[]{:S(2)}, u32[]{:S(2)}) collective-permute-start(f32[1,1,4,64,128]{4,3,2,1,0:T(8,128)S(1)} %bitcast_subtract_fusion.1), channel_id=1, source_target_pairs={{64,0},{128,64},{192,128},{256,192},{320,256},{384,320},{448,384},... | collective-permute-start | bytes 393224 | tf_op jit(solution)/shard_map/ppermute | solution.py:21
  265.2 9.4 %collective-permute-start.10 = (f32[1,1,4,64,128]{4,3,2,1,0:T(8,128)S(1)}, f32[1,1,4,64,128]{4,3,2,1,0:T(8,128)S(1)}, u32[]{:S(2)}, u32[]{:S(2)}) collective-permute-start(f32[1,1,4,64,128]{4,3,2,1,0:T(8,128)S(1)} %bitcast_subtract_fusion.1), channel_id=1, source_target_pairs={{0,1},{1,2},{2,3},{3,4},{4,5},{5,6},{6,7},{7,8},{8,9},{9,10},{10,1... | collective-permute-start | bytes 393224 | tf_op jit(solution)/shard_map/ppermute | solution.py:20
  270.9 5.6 collective-permute-start.8
  302.4 17.8 %all-to-all-start.3 = ((f32[16,1,1152]{2,1,0:T(1,128)}), f32[16,1,1152]{2,1,0:T(1,128)S(1)}, u32[]{:S(2)}, u32[]{:S(2)}) async-start(f32[16,1,1152]{2,1,0:T(1,128)} %reshape.1347), calls=%async_computation.3 | async-start | bytes 147456 | tf_op jit(solution)/shard_map/all_to_all | solution.py:46
  312.3 162.6 %all-reduce.6.cloned.1.call-start = ((), (), s32[]{:S(2)}) async-start(), calls=%async_computation.7 | async-start | bytes 589824 | tf_op jit(solution)/shard_map/psum | solution.py:83
  476.4 16.5 %collective-permute-start.14 = (f32[1,1,4,64,128]{4,3,2,1,0:T(8,128)S(1)}, f32[1,1,4,64,128]{4,3,2,1,0:T(8,128)S(1)}, u32[]{:S(2)}, u32[]{:S(2)}) collective-permute-start(f32[1,1,4,64,128]{4,3,2,1,0:T(8,128)S(1)} %fusion.3), channel_id=1, source_target_pairs={{0,1},{1,2},{2,3},{3,4},{4,5},{5,6},{6,7},{7,8},{8,9},{9,10},{10,1... | collective-permute-start | bytes 393224 | tf_op jit(solution)/shard_map/ppermute | solution.py:20
  480.7 12.2 %collective-permute-start.13 = (f32[1,1,4,64,128]{4,3,2,1,0:T(8,128)S(1)}, f32[1,1,4,64,128]{4,3,2,1,0:T(8,128)S(1)}, u32[]{:S(2)}, u32[]{:S(2)}) collective-permute-start(f32[1,1,4,64,128]{4,3,2,1,0:T(8,128)S(1)} %fusion.3), channel_id=1, source_target_pairs={{64,0},{128,64},{192,128},{256,192},{320,256},{384,320},{448,384},... | collective-permute-start | bytes 393224 | tf_op jit(solution)/shard_map/ppermute | solution.py:21
  487.6 5.3 collective-permute-start.12
  491.0 8.8 %collective-permute-start.15 = (f32[1,1,4,64,128]{4,3,2,1,0:T(8,128)S(1)}, f32[1,1,4,64,128]{4,3,2,1,0:T(8,128)S(1)}, u32[]{:S(2)}, u32[]{:S(2)}) collective-permute-start(f32[1,1,4,64,128]{4,3,2,1,0:T(8,128)S(1)} %fusion.3), channel_id=1, source_target_pairs={{1,0},{2,1},{3,2},{4,3},{5,4},{6,5},{7,6},{8,7},{9,8},{10,9},{11,1... | collective-permute-start | bytes 393224 | tf_op jit(solution)/shard_map/ppermute | solution.py:21
  500.7 13.5 %collective-permute-start.19 = (f32[1,1,4,64,128]{4,3,2,1,0:T(8,128)S(1)}, f32[1,1,4,64,128]{4,3,2,1,0:T(8,128)S(1)}, u32[]{:S(2)}, u32[]{:S(2)}) collective-permute-start(f32[1,1,4,64,128]{4,3,2,1,0:T(8,128)S(1)} %bitcast_subtract_fusion), channel_id=1, source_target_pairs={{1,0},{2,1},{3,2},{4,3},{5,4},{6,5},{7,6},{8,7},{9,8},{10,9},{11,1... | collective-permute-start | bytes 393224 | tf_op jit(solution)/shard_map/ppermute | solution.py:21
  502.6 11.5 %collective-permute-start.17 = (f32[1,1,4,64,128]{4,3,2,1,0:T(8,128)S(1)}, f32[1,1,4,64,128]{4,3,2,1,0:T(8,128)S(1)}, u32[]{:S(2)}, u32[]{:S(2)}) collective-permute-start(f32[1,1,4,64,128]{4,3,2,1,0:T(8,128)S(1)} %bitcast_subtract_fusion), channel_id=1, source_target_pairs={{64,0},{128,64},{192,128},{256,192},{320,256},{384,320},{448,384},... | collective-permute-start | bytes 393224 | tf_op jit(solution)/shard_map/ppermute | solution.py:21
  504.8 9.4 %collective-permute-start.18 = (f32[1,1,4,64,128]{4,3,2,1,0:T(8,128)S(1)}, f32[1,1,4,64,128]{4,3,2,1,0:T(8,128)S(1)}, u32[]{:S(2)}, u32[]{:S(2)}) collective-permute-start(f32[1,1,4,64,128]{4,3,2,1,0:T(8,128)S(1)} %bitcast_subtract_fusion), channel_id=1, source_target_pairs={{0,1},{1,2},{2,3},{3,4},{4,5},{5,6},{6,7},{7,8},{8,9},{9,10},{10,1... | collective-permute-start | bytes 393224 | tf_op jit(solution)/shard_map/ppermute | solution.py:20
  510.5 5.6 collective-permute-start.16
  542.0 17.8 %all-to-all-start.5 = ((f32[16,1,1152]{2,1,0:T(1,128)}), f32[16,1,1152]{2,1,0:T(1,128)S(1)}, u32[]{:S(2)}, u32[]{:S(2)}) async-start(f32[16,1,1152]{2,1,0:T(1,128)} %reshape.1351), calls=%async_computation.5 | async-start | bytes 147456 | tf_op jit(solution)/shard_map/all_to_all | solution.py:46
  551.9 162.5 %all-reduce.8.cloned.1.call-start = ((), (), s32[]{:S(2)}) async-start(), calls=%async_computation.8 | async-start | bytes 589824 | tf_op jit(solution)/shard_map/psum | solution.py:83
  716.0 18.3 %collective-permute-start.23 = (f32[1,1,4,64,128]{4,3,2,1,0:T(8,128)S(1)}, f32[1,1,4,64,128]{4,3,2,1,0:T(8,128)S(1)}, u32[]{:S(2)}, u32[]{:S(2)}) collective-permute-start(f32[1,1,4,64,128]{4,3,2,1,0:T(8,128)S(1)} %fusion.5), channel_id=1, source_target_pairs={{1,0},{2,1},{3,2},{4,3},{5,4},{6,5},{7,6},{8,7},{9,8},{10,9},{11,1... | collective-permute-start | bytes 393224 | tf_op jit(solution)/shard_map/ppermute | solution.py:21
  718.5 15.8 %collective-permute-start.21 = (f32[1,1,4,64,128]{4,3,2,1,0:T(8,128)S(1)}, f32[1,1,4,64,128]{4,3,2,1,0:T(8,128)S(1)}, u32[]{:S(2)}, u32[]{:S(2)}) collective-permute-start(f32[1,1,4,64,128]{4,3,2,1,0:T(8,128)S(1)} %fusion.5), channel_id=1, source_target_pairs={{64,0},{128,64},{192,128},{256,192},{320,256},{384,320},{448,384},... | collective-permute-start | bytes 393224 | tf_op jit(solution)/shard_map/ppermute | solution.py:21
  725.7 8.7 %collective-permute-start.22 = (f32[1,1,4,64,128]{4,3,2,1,0:T(8,128)S(1)}, f32[1,1,4,64,128]{4,3,2,1,0:T(8,128)S(1)}, u32[]{:S(2)}, u32[]{:S(2)}) collective-permute-start(f32[1,1,4,64,128]{4,3,2,1,0:T(8,128)S(1)} %fusion.5), channel_id=1, source_target_pairs={{0,1},{1,2},{2,3},{3,4},{4,5},{5,6},{6,7},{7,8},{8,9},{9,10},{10,1... | collective-permute-start | bytes 393224 | tf_op jit(solution)/shard_map/ppermute | solution.py:20
  730.7 5.6 collective-permute-start.20
Sparse Core Ops, SparseCore 0:
  83.2 152.0 all-reduce.3
  322.5 152.2 all-reduce.5
  562.1 152.2 all-reduce.7
where the time goes:
time: 745 us; the launch traced here: 743 us
  waiting for transfers between devices  511 us (69%)
  starting transfers between devices  142 us (19%)
  blocking collectives  43.9 us (6%)
  matrix products  15.3 us (2%)
  between operations  13.9 us (2%)
  local copies, waits for them, and re-layouts  9.91 us (1%)
  other arithmetic  8.29 us (1%)
    psum x3, waiting for transfers between devices, coarse_solve(): return lax.psum(owned_term, 'wide')  455 us
    ppermute x12, starting transfers between devices, padded_2(): lax.ppermute(last, axis, up)  50.9 us
    all_to_all x2, blocking collectives, sum_at_owner(): tiles = lax.all_to_all(split_up(array, dim, peers), axis, 0, 0, tiled=True)  43.9 us
    ppermute x12, starting transfers between devices, padded_2(): lax.ppermute(first, axis, [(b, a) for a, b in up])  40.4 us
    all_to_all x3, starting transfers between devices, copy_for_each(): lax.all_to_all(jnp.broadcast_to(array[None], (peers, *array.shape)), axis...  35.8 us
    all_to_all x3, waiting for transfers between devices, copy_for_each(): lax.all_to_all(jnp.broadcast_to(array[None], (peers, *array.shape)), axis...  21.8 us
    ppermute x12, waiting for transfers between devices, padded_2(): lax.ppermute(first, axis, [(b, a) for a, b in up])  15.2 us
  transfers between devices with their start and end apart: 31, of which 13 were waited for; matrix products, arithmetic and copies ran while one was open for 0% of the time, Pallas kernels for 0%

commit v1 on v0

v1 whole, which is shorter than its diff:
```python
import jax
import jax.numpy as jnp
from jax import lax
from jax.sharding import PartitionSpec as P

ITERS = 3
damping = 0.3
HIGHEST = lax.Precision.HIGHEST


def assemble(faces):
    rows = lax.axis_size("sub")
    cols = lax.axis_size("wide")
    down = [(i, i + 1) for i in range(rows - 1)]
    right = [(i, i + 1) for i in range(cols - 1)]
    from_north = lax.ppermute(faces[1], "sub", down)
    from_south = lax.ppermute(faces[0], "sub", [(b, a) for a, b in down])
    from_west = lax.ppermute(faces[3], "wide", right)
    from_east = lax.ppermute(faces[2], "wide", [(b, a) for a, b in right])
    return faces + jnp.stack([from_north, from_south, from_west, from_east])


def apply_local(faces, operator, selector_half, selector_full):
    rhs, width = faces.shape[1:]
    blocked = jnp.einsum(
        "bf,fjn->jbn", selector_half, faces.astype(jnp.bfloat16), preferred_element_type=jnp.float32
    )
    blocked = blocked.astype(jnp.bfloat16).reshape(rhs, 4 * width)
    product = jnp.dot(blocked, operator, preferred_element_type=jnp.float32)
    product = product.reshape(rhs, 4, width)
    return jnp.einsum("bf,jbn->fjn", selector_full, product, precision=HIGHEST)


def in_three(array):
    high = lax.reduce_precision(array, 8, 7)
    rest = array - high
    middle = lax.reduce_precision(rest, 8, 7)
    low = lax.reduce_precision(rest - middle, 8, 7)
    return high.astype(jnp.bfloat16), middle.astype(jnp.bfloat16), low.astype(jnp.bfloat16)


def pick_columns(matrix, ids):
    parts = jnp.concatenate(in_three(matrix), axis=0)
    order = matrix.shape[1]
    marks = (jnp.arange(order, dtype=jnp.int32)[:, None] == ids[None, :]).astype(jnp.bfloat16)
    picked = jnp.dot(parts, marks, preferred_element_type=jnp.float32)
    high, middle, low = jnp.split(picked, 3, axis=0)
    return (high + middle) + low


def own_inverse_rows(corner_ids, coarse_inverse):
    peers = lax.axis_size("wide")
    owned = coarse_inverse.shape[0]
    prims = corner_ids.shape[0]
    id_row = jnp.pad(corner_ids.astype(jnp.float32), (0, 128 - prims))[None, :]
    ids = lax.all_gather(id_row, "wide")[:, 0, :prims].astype(jnp.int32).reshape(-1)
    entries = pick_columns(coarse_inverse, ids)
    entries = entries.reshape(owned, peers, prims).transpose(1, 2, 0).reshape(peers, prims * owned)
    entries = lax.all_to_all(entries, "wide", 0, 0, tiled=True)
    entries = entries.reshape(peers, prims, owned).transpose(1, 0, 2)
    return entries.reshape(prims, peers * owned)


def slots_of_column(ids, amount):
    count = ids.shape[0]
    place = jnp.arange(count, dtype=jnp.int32)
    same = ids[:, None] == ids[None, :]
    first = ~jnp.any(same & (place[None, :] < place[:, None]), axis=1)
    rank_of_first = jnp.sum(first[None, :] & (place[None, :] < place[:, None]), axis=1)
    rank = jnp.sum(jnp.where(same & first[None, :], rank_of_first[None, :], 0), axis=1)
    slots = rank[None, :] == jnp.arange(amount, dtype=jnp.int32)[:, None]
    slot_ids = jnp.max(jnp.where(slots, ids[None, :], 0.0), axis=1)
    return slots.astype(jnp.float32), slot_ids


def body(
    load_table, load_column, face_order, schur, neumann, coarse_basis, corner_map, coarse_inverse
):
    load_table, face_order, schur, neumann, coarse_basis, corner_ids = (
        a[0, 0] for a in (load_table, face_order, schur, neumann, coarse_basis, corner_map)
    )
    patterns = load_table.shape[0]
    prims = corner_ids.shape[0]
    rhs = load_column.shape[0]
    rows_total = lax.axis_size("sub")
    cols_total = lax.axis_size("wide")
    half_slots = rows_total + 1
    selector_full = (face_order[:, None] == jnp.arange(4, dtype=jnp.int32)).astype(jnp.float32)
    selector_half = selector_full.astype(jnp.bfloat16)
    load_select = (load_column[:, None] == jnp.arange(patterns, dtype=jnp.int32)).astype(
        jnp.bfloat16
    )
    load_faces = jnp.einsum(
        "jl,lfn->fjn", load_select, load_table, preferred_element_type=jnp.float32
    )
    row = lax.axis_index("sub")
    col = lax.axis_index("wide")
    inner = jnp.stack([row > 0, row < rows_total - 1, col > 0, col < cols_total - 1])
    weights = jnp.where(inner, jnp.float32(0.5), jnp.float32(1.0))[:, None, None]
    basis = coarse_basis.astype(jnp.float32)
    inverse_rows = own_inverse_rows(corner_ids, coarse_inverse)
    id_lanes = jnp.broadcast_to(corner_ids.astype(jnp.float32)[:, None], (prims, rhs))
    solution = jnp.zeros(load_faces.shape, jnp.float32)
    for iteration in range(ITERS):
        if iteration == 0:
            residual = assemble(load_faces)
        else:
            residual = assemble(
                load_faces - apply_local(solution, schur, selector_half, selector_full)
            )
        weighted = weights * residual
        restricted = jnp.einsum("pfn,fjn->pj", basis, weighted, precision=HIGHEST)
        in_column = lax.all_gather(
            jnp.concatenate([restricted, id_lanes], axis=1), "sub", axis=0, tiled=True
        )
        if iteration == 0:
            slots, slot_ids = slots_of_column(in_column[:, rhs], 2 * half_slots)
        summed = jnp.dot(slots, in_column[:, :rhs], precision=HIGHEST)
        summed = jnp.concatenate([summed[:half_slots], summed[half_slots:]], axis=1)
        if iteration == 0:
            id_row = jnp.pad(slot_ids, (0, 2 * rhs - 2 * half_slots))[None, :]
            everyone = lax.all_gather(jnp.concatenate([summed, id_row]), "wide")
            ids = everyone[:, half_slots, : 2 * half_slots].astype(jnp.int32)
            everyone = everyone[:, :half_slots]
            ids = ids.reshape(cols_total, 2, half_slots).transpose(1, 0, 2).reshape(-1)
            rows_at = pick_columns(inverse_rows, ids)
            rows_at = rows_at.reshape(prims, 2, cols_total * half_slots)
            rows_at = rows_at.transpose(1, 0, 2).reshape(2 * prims, -1)
        else:
            everyone = lax.all_gather(summed, "wide")
        solved = jnp.dot(
            rows_at, everyone.reshape(cols_total * half_slots, 2 * rhs), precision=HIGHEST
        )
        picked = solved[:prims, :rhs] + solved[prims:, rhs:]
        neumann_part = apply_local(weighted, neumann, selector_half, selector_full)
        correction = jnp.einsum("pj,pfn->fjn", picked, basis, precision=HIGHEST)
        update = assemble(weights * (neumann_part + correction))
        solution = solution + damping * update
    return solution[None, None]


def solution(mesh):
    in_specs = (
        P("sub", "wide", None, None, None),
        P(),
        P("sub", "wide", None),
        P("sub", "wide", None, None),
        P("sub", "wide", None, None),
        P("sub", "wide", None, None, None),
        P("sub", "wide", None),
        P("wide", None),
    )
    out_specs = P("sub", "wide", None, None, None)
    return jax.shard_map(body, mesh=mesh, in_specs=in_specs, out_specs=out_specs, check_vma=False)
```

time: 745 us -> 372 us (0.50)
  waiting for transfers between devices: 511 us -> 13.6 us
  blocking collectives: 43.9 us -> 222 us
  starting transfers between devices: 142 us -> 116 us
  between operations: 13.9 us -> 0.86 us
    psum x3 -> x0, waiting for transfers between devices: 455 us -> none  [coarse_solve(): return lax.psum(owned_term, 'wide')]
    all_gather x0 -> x7, blocking collectives: none -> 222 us  [the longest x2 78.8 us: body(): everyone = lax.all_gather(summed, 'wide')]
    all_to_all x2 -> x0, blocking collectives: 43.9 us -> none  [sum_at_owner(): tiles = lax.all_to_all(split_up(array, dim, peers), axis, 0, 0, tiled=True)]
    all_to_all x4 -> x1, starting transfers between devices: 50 us -> 8.15 us  [own_inverse_rows(): entries = lax.all_to_all(entries, 'wide', 0, 0, tiled=True)]
    all_to_all x4 -> x1, waiting for transfers between devices: 34.3 us -> 0.01 us  [own_inverse_rows(): entries = lax.all_to_all(entries, 'wide', 0, 0, tiled=True)]
    ppermute x24, starting transfers between devices: 91.3 us -> 108 us  [the longest x6 47.6 us: assemble(): from_north = lax.ppermute(faces[1], 'sub', down)]
    dot_general x31 -> x30, matrix products: 15.3 us -> 10.4 us  [the longest x2 2.18 us: pick_columns(): picked = jnp.dot(parts, marks, preferred_element_type=jnp.float32)]
  transfers between devices with their start and end apart: 31 -> 25, of which waited for: 13 -> 5; matrix products, arithmetic and copies ran while one was open for 0% -> 2% of each run, Pallas kernels for 0% -> 0%
where the time goes in v1:
time: 372 us; the launch traced here: 370 us
  blocking collectives  222 us (60%)
  starting transfers between devices  116 us (31%)
  waiting for transfers between devices  13.6 us (4%)
  matrix products  10.4 us (3%)
  other arithmetic  4.11 us (1%)
    all_gather x2, blocking collectives, body(): everyone = lax.all_gather(summed, 'wide')  78.8 us
    all_gather x3, blocking collectives, body(): lax.all_gather(jnp.concatenate([restricted, id_lanes], axis=1), 'sub', ax...  69.3 us
    ppermute x6, starting transfers between devices, assemble(): from_north = lax.ppermute(faces[1], 'sub', down)  47.6 us
    all_gather x1, blocking collectives, body(): everyone = lax.all_gather(jnp.concatenate([summed, id_row]), 'wide')  38.7 us
    all_gather x1, blocking collectives, own_inverse_rows(): lax.all_gather(id_row, 'wide')[:, 0, :prims].astype(jnp.int32).reshape(-1)  35 us
    ppermute x6, starting transfers between devices, assemble(): from_west = lax.ppermute(faces[3], 'wide', right)  31.1 us
    ppermute x6, starting transfers between devices, assemble(): from_south = lax.ppermute(faces[0], 'sub', [(b, a) for a, b in down])  15.8 us
    ppermute x6, waiting for transfers between devices, assemble(): from_south = lax.ppermute(faces[0], 'sub', [(b, a) for a, b in down])  13.5 us
  transfers between devices with their start and end apart: 25, of which 5 were waited for; matrix products, arithmetic and copies ran while one was open for 2% of the time, Pallas kernels for 0%

profile of v1, /device:TPU:15, one launch (start us, length us, event | category | flops | bytes accessed | tf_op | source)
XLA Modules:
  0.0 370.4 jit_solution(8512862743047629674)
XLA Ops:
  0.0 0.7 copy-done
  0.7 0.9 convolution_bitcast_fusion.3
  1.6 5.5 %collective-permute-start = (f32[64,128]{1,0:T(8,128)S(1)}, f32[64,128]{1,0:T(8,128)S(1)}, u32[]{:S(2)}, u32[]{:S(2)}) collective-permute-start(f32[64,128]{1,0:T(8,128)S(1)} %get-tuple-element.27), channel_id=1, source_target_pairs={{0,64},{64,128},{128,192},{192,256},{256,320},{320,384},{384,448},... | collective-permute-start | bytes 98312 | tf_op jit(solution)/shard_map/ppermute | solution.py:16
  7.1 3.1 collective-permute-start.3
  10.1 4.3 %collective-permute-start.2 = (f32[64,128]{1,0:T(8,128)S(1)}, f32[64,128]{1,0:T(8,128)S(1)}, u32[]{:S(2)}, u32[]{:S(2)}) collective-permute-start(f32[64,128]{1,0:T(8,128)S(1)} %get-tuple-element.29), channel_id=1, source_target_pairs={{0,1},{1,2},{2,3},{3,4},{4,5},{5,6},{6,7},{7,8},{8,9},{9,10},{10,1... | collective-permute-start | bytes 98312 | tf_op jit(solution)/shard_map/ppermute | solution.py:18
  14.5 1.9 collective-permute-start.1
  16.4 0.7 convert_bitcast_fusion
  17.1 35.0 %all-gather.4 = f32[64,1,128]{2,1,0:T(1,128)S(1)} all-gather(f32[1,1,128]{2,1,0:T(1,128)S(1)} %pad_bitcast_fusion.1), channel_id=2, replica_groups=mesh['sub'=16,'wide'=64] {'wide'}, dimensions={0}, use_global_device_ids=true | all-gather | bytes 33280 | tf_op jit(solution)/shard_map/all_gather | solution.py:56
  52.3 1.0 reduce-precision_convert_fusion.1
  53.2 0.4 fusion.2
  53.7 0.7 reshape.165
  54.5 8.1 %all-to-all-start = ((f32[64,1,72]{2,1,0:T(1,128)}), f32[64,1,72]{2,1,0:T(1,128)S(1)}, u32[]{:S(2)}, u32[]{:S(2)}) async-start(f32[64,1,72]{2,1,0:T(1,128)} %bitcast.106), calls=%async_computation | async-start | bytes 65536 | tf_op jit(solution)/shard_map/all_to_all | solution.py:59
  63.4 37.8 %all-gather.5 = f32[16,4,128]{2,1,0:T(4,128)S(1)} all-gather(f32[1,4,128]{2,1,0:T(4,128)S(1)} %fusion.69), channel_id=1, replica_groups=mesh['sub'=16,'wide'=64] {'sub'}, dimensions={0}, use_global_device_ids=true | all-gather | bytes 34816 | tf_op jit(solution)/shard_map/all_gather | solution.py:113
  102.2 0.2 fusion.9
  102.5 0.3 fusion.121
  102.7 0.3 fusion.32
  103.2 38.7 %all-gather.6 = f32[64,18,128]{2,1,0:T(8,128)S(1)} all-gather(f32[1,18,128]{2,1,0:T(8,128)S(1)} %maximum_bitcast_fusion), channel_id=3, replica_groups=mesh['sub'=16,'wide'=64] {'wide'}, dimensions={0}, use_global_device_ids=true | all-gather | bytes 599040 | tf_op jit(solution)/shard_map/all_gather | solution.py:122
  142.8 1.8 fusion
  144.8 0.4 fusion.122
  145.1 0.4 fusion.4
  145.5 12.0 %collective-permute-start.4 = (f32[64,128]{1,0:T(8,128)S(1)}, f32[64,128]{1,0:T(8,128)S(1)}, u32[]{:S(2)}, u32[]{:S(2)}) collective-permute-start(f32[64,128]{1,0:T(8,128)S(1)} %get-tuple-element.23), channel_id=1, source_target_pairs={{0,64},{64,128},{128,192},{192,256},{256,320},{320,384},{384,448},... | collective-permute-start | bytes 98312 | tf_op jit(solution)/shard_map/ppermute | solution.py:16
  157.5 2.7 collective-permute-start.7
  160.2 4.7 %collective-permute-start.6 = (f32[64,128]{1,0:T(8,128)S(1)}, f32[64,128]{1,0:T(8,128)S(1)}, u32[]{:S(2)}, u32[]{:S(2)}) collective-permute-start(f32[64,128]{1,0:T(8,128)S(1)} %get-tuple-element.25), channel_id=1, source_target_pairs={{0,1},{1,2},{2,3},{3,4},{4,5},{5,6},{6,7},{7,8},{8,9},{9,10},{10,1... | collective-permute-start | bytes 98312 | tf_op jit(solution)/shard_map/ppermute | solution.py:18
  164.9 3.4 collective-permute-start.5
  168.6 1.5 collective-permute-done.5
  170.2 0.2 fusion.10
  170.4 0.3 fusion.123
  170.7 0.3 fusion.30
  171.1 1.9 collective-permute-start.8
  173.0 1.9 collective-permute-start.11
  174.9 5.5 %collective-permute-start.10 = (f32[64,128]{1,0:T(8,128)S(1)}, f32[64,128]{1,0:T(8,128)S(1)}, u32[]{:S(2)}, u32[]{:S(2)}) collective-permute-start(f32[64,128]{1,0:T(8,128)S(1)} %get-tuple-element.21), channel_id=1, source_target_pairs={{0,1},{1,2},{2,3},{3,4},{4,5},{5,6},{6,7},{7,8},{8,9},{9,10},{10,1... | collective-permute-start | bytes 98312 | tf_op jit(solution)/shard_map/ppermute | solution.py:18
  180.4 3.0 collective-permute-start.9
  183.4 3.2 collective-permute-done.9
  187.3 14.5 %all-gather.7 = f32[16,4,128]{2,1,0:T(4,128)S(1)} all-gather(f32[1,4,128]{2,1,0:T(4,128)S(1)} %fusion.70), channel_id=1, replica_groups=mesh['sub'=16,'wide'=64] {'sub'}, dimensions={0}, use_global_device_ids=true | all-gather | bytes 34816 | tf_op jit(solution)/shard_map/all_gather | solution.py:113
  202.0 0.3 fusion.124
  202.2 0.3 fusion.28
  202.6 39.6 %all-gather.8 = f32[64,17,128]{2,1,0:T(8,128)S(1)} all-gather(f32[1,17,128]{2,1,0:T(8,128)S(1)} %maximum_bitcast_fusion.1), channel_id=4, replica_groups=mesh['sub'=16,'wide'=64] {'wide'}, dimensions={0}, use_global_device_ids=true | all-gather | bytes 565760 | tf_op jit(solution)/shard_map/all_gather | solution.py:130
  242.3 0.4 fusion.125
  242.7 0.4 fusion.6
  243.1 13.4 %collective-permute-start.12 = (f32[64,128]{1,0:T(8,128)S(1)}, f32[64,128]{1,0:T(8,128)S(1)}, u32[]{:S(2)}, u32[]{:S(2)}) collective-permute-start(f32[64,128]{1,0:T(8,128)S(1)} %get-tuple-element.15), channel_id=1, source_target_pairs={{0,64},{64,128},{128,192},{192,256},{256,320},{320,384},{384,448},... | collective-permute-start | bytes 98312 | tf_op jit(solution)/shard_map/ppermute | solution.py:16
  256.5 1.9 collective-permute-start.15
  258.4 5.5 %collective-permute-start.14 = (f32[64,128]{1,0:T(8,128)S(1)}, f32[64,128]{1,0:T(8,128)S(1)}, u32[]{:S(2)}, u32[]{:S(2)}) collective-permute-start(f32[64,128]{1,0:T(8,128)S(1)} %get-tuple-element.17), channel_id=1, source_target_pairs={{0,1},{1,2},{2,3},{3,4},{4,5},{5,6},{6,7},{7,8},{8,9},{9,10},{10,1... | collective-permute-start | bytes 98312 | tf_op jit(solution)/shard_map/ppermute | solution.py:18
  263.9 2.3 collective-permute-start.13
  266.2 2.9 collective-permute-done.13
  269.2 0.2 fusion.12
  269.4 0.3 fusion.126
  269.7 0.3 fusion.26
  270.1 1.9 collective-permute-start.16
  272.0 1.9 collective-permute-start.19
  274.0 5.7 %collective-permute-start.18 = (f32[64,128]{1,0:T(8,128)S(1)}, f32[64,128]{1,0:T(8,128)S(1)}, u32[]{:S(2)}, u32[]{:S(2)}) collective-permute-start(f32[64,128]{1,0:T(8,128)S(1)} %get-tuple-element.13), channel_id=1, source_target_pairs={{0,1},{1,2},{2,3},{3,4},{4,5},{5,6},{6,7},{7,8},{8,9},{9,10},{10,1... | collective-permute-start | bytes 98312 | tf_op jit(solution)/shard_map/ppermute | solution.py:18
  279.6 3.0 collective-permute-start.17
  282.6 3.0 collective-permute-done.17
  286.3 0.3 fusion.127
  286.6 0.3 fusion.24
  286.9 17.0 %all-gather.9 = f32[16,4,128]{2,1,0:T(4,128)S(1)} all-gather(f32[1,4,128]{2,1,0:T(4,128)S(1)} %fusion.71), channel_id=1, replica_groups=mesh['sub'=16,'wide'=64] {'sub'}, dimensions={0}, use_global_device_ids=true | all-gather | bytes 34816 | tf_op jit(solution)/shard_map/all_gather | solution.py:113
  304.1 39.2 %all-gather.10 = f32[64,17,128]{2,1,0:T(8,128)S(1)} all-gather(f32[1,17,128]{2,1,0:T(8,128)S(1)} %maximum_bitcast_fusion.2), channel_id=5, replica_groups=mesh['sub'=16,'wide'=64] {'wide'}, dimensions={0}, use_global_device_ids=true | all-gather | bytes 565760 | tf_op jit(solution)/shard_map/all_gather | solution.py:130
  343.4 0.4 fusion.128
  343.8 0.4 fusion.8
  344.2 12.9 %collective-permute-start.20 = (f32[64,128]{1,0:T(8,128)S(1)}, f32[64,128]{1,0:T(8,128)S(1)}, u32[]{:S(2)}, u32[]{:S(2)}) collective-permute-start(f32[64,128]{1,0:T(8,128)S(1)} %get-tuple-element.7), channel_id=1, source_target_pairs={{0,64},{64,128},{128,192},{192,256},{256,320},{320,384},{384,448},... | collective-permute-start | bytes 98312 | tf_op jit(solution)/shard_map/ppermute | solution.py:16
  357.1 1.9 collective-permute-start.23
  359.0 5.5 %collective-permute-start.22 = (f32[64,128]{1,0:T(8,128)S(1)}, f32[64,128]{1,0:T(8,128)S(1)}, u32[]{:S(2)}, u32[]{:S(2)}) collective-permute-start(f32[64,128]{1,0:T(8,128)S(1)} %get-tuple-element.9), channel_id=1, source_target_pairs={{0,1},{1,2},{2,3},{3,4},{4,5},{5,6},{6,7},{7,8},{8,9},{9,10},{10,1... | collective-permute-start | bytes 98312 | tf_op jit(solution)/shard_map/ppermute | solution.py:18
  364.5 2.3 collective-permute-start.21
  366.8 2.9 collective-permute-done.21
  369.7 0.7 fusion.23
  (99 shorter events, 5.5 us)
Async XLA Ops:
  0.0 0.7 copy-start
  1.6 61.3 %collective-permute-start = (f32[64,128]{1,0:T(8,128)S(1)}, f32[64,128]{1,0:T(8,128)S(1)}, u32[]{:S(2)}, u32[]{:S(2)}) collective-permute-start(f32[64,128]{1,0:T(8,128)S(1)} %get-tuple-element.27), channel_id=1, source_target_pairs={{0,64},{64,128},{128,192},{192,256},{256,320},{320,384},{384,448},... | collective-permute-start | bytes 98312 | tf_op jit(solution)/shard_map/ppermute | solution.py:16
  7.1 55.9 %collective-permute-start.3 = (f32[64,128]{1,0:T(8,128)S(1)}, f32[64,128]{1,0:T(8,128)S(1)}, u32[]{:S(2)}, u32[]{:S(2)}) collective-permute-start(f32[64,128]{1,0:T(8,128)S(1)} %get-tuple-element.28), channel_id=1, source_target_pairs={{1,0},{2,1},{3,2},{4,3},{5,4},{6,5},{7,6},{8,7},{9,8},{10,9},{11,1... | collective-permute-start | bytes 98312 | tf_op jit(solution)/shard_map/ppermute | solution.py:19
  10.1 52.8 %collective-permute-start.2 = (f32[64,128]{1,0:T(8,128)S(1)}, f32[64,128]{1,0:T(8,128)S(1)}, u32[]{:S(2)}, u32[]{:S(2)}) collective-permute-start(f32[64,128]{1,0:T(8,128)S(1)} %get-tuple-element.29), channel_id=1, source_target_pairs={{0,1},{1,2},{2,3},{3,4},{4,5},{5,6},{6,7},{7,8},{8,9},{9,10},{10,1... | collective-permute-start | bytes 98312 | tf_op jit(solution)/shard_map/ppermute | solution.py:18
  14.5 48.5 %collective-permute-start.1 = (f32[64,128]{1,0:T(8,128)S(1)}, f32[64,128]{1,0:T(8,128)S(1)}, u32[]{:S(2)}, u32[]{:S(2)}) collective-permute-start(f32[64,128]{1,0:T(8,128)S(1)} %get-tuple-element.30), channel_id=1, source_target_pairs={{64,0},{128,64},{192,128},{256,192},{320,256},{384,320},{448,384},... | collective-permute-start | bytes 98312 | tf_op jit(solution)/shard_map/ppermute | solution.py:17
  52.1 10.6 %copy-start.1 = (bf16[1,1,512,512]{3,2,1,0:T(8,128)(2,1)S(1)}, bf16[1,1,512,512]{3,2,1,0:T(8,128)(2,1)}, u32[]{:S(2)}) copy-start(bf16[1,1,512,512]{3,2,1,0:T(8,128)(2,1)} %param.12) | copy-start | bytes 1572868
  53.7 9.3 %copy-start.3 = (bf16[1,1,4,4,128]{4,3,2,1,0:T(4,128)(2,1)S(1)}, bf16[1,1,4,4,128]{4,3,2,1,0:T(4,128)(2,1)}, u32[]{:S(2)}) copy-start(bf16[1,1,4,4,128]{4,3,2,1,0:T(4,128)(2,1)} %param.13) | copy-start | bytes 12292
  54.5 87.9 %all-to-all-start = ((f32[64,1,72]{2,1,0:T(1,128)}), f32[64,1,72]{2,1,0:T(1,128)S(1)}, u32[]{:S(2)}, u32[]{:S(2)}) async-start(f32[64,1,72]{2,1,0:T(1,128)} %bitcast.106), calls=%async_computation | async-start | bytes 65536 | tf_op jit(solution)/shard_map/all_to_all | solution.py:59
  62.7 39.4 %copy-start.4 = (s32[1,1,4]{2,1,0:T(1,128)S(1)}, s32[1,1,4]{2,1,0:T(1,128)}, u32[]{:S(2)}) copy-start(s32[1,1,4]{2,1,0:T(1,128)} %param.10) | copy-start | bytes 52
  144.6 23.7 %copy-start.2 = (bf16[1,1,512,512]{3,2,1,0:T(8,128)(2,1)S(1)}, bf16[1,1,512,512]{3,2,1,0:T(8,128)(2,1)}, u32[]{:S(2)}) copy-start(bf16[1,1,512,512]{3,2,1,0:T(8,128)(2,1)} %param.11) | copy-start | bytes 1572868
  145.5 23.0 %collective-permute-start.4 = (f32[64,128]{1,0:T(8,128)S(1)}, f32[64,128]{1,0:T(8,128)S(1)}, u32[]{:S(2)}, u32[]{:S(2)}) collective-permute-start(f32[64,128]{1,0:T(8,128)S(1)} %get-tuple-element.23), channel_id=1, source_target_pairs={{0,64},{64,128},{128,192},{192,256},{256,320},{320,384},{384,448},... | collective-permute-start | bytes 98312 | tf_op jit(solution)/shard_map/ppermute | solution.py:16
  157.5 11.1 %collective-permute-start.7 = (f32[64,128]{1,0:T(8,128)S(1)}, f32[64,128]{1,0:T(8,128)S(1)}, u32[]{:S(2)}, u32[]{:S(2)}) collective-permute-start(f32[64,128]{1,0:T(8,128)S(1)} %get-tuple-element.24), channel_id=1, source_target_pairs={{1,0},{2,1},{3,2},{4,3},{5,4},{6,5},{7,6},{8,7},{9,8},{10,9},{11,1... | collective-permute-start | bytes 98312 | tf_op jit(solution)/shard_map/ppermute | solution.py:19
  160.2 8.4 %collective-permute-start.6 = (f32[64,128]{1,0:T(8,128)S(1)}, f32[64,128]{1,0:T(8,128)S(1)}, u32[]{:S(2)}, u32[]{:S(2)}) collective-permute-start(f32[64,128]{1,0:T(8,128)S(1)} %get-tuple-element.25), channel_id=1, source_target_pairs={{0,1},{1,2},{2,3},{3,4},{4,5},{5,6},{6,7},{7,8},{8,9},{9,10},{10,1... | collective-permute-start | bytes 98312 | tf_op jit(solution)/shard_map/ppermute | solution.py:18
  164.9 5.2 %collective-permute-start.5 = (f32[64,128]{1,0:T(8,128)S(1)}, f32[64,128]{1,0:T(8,128)S(1)}, u32[]{:S(2)}, u32[]{:S(2)}) collective-permute-start(f32[64,128]{1,0:T(8,128)S(1)} %get-tuple-element.26), channel_id=1, source_target_pairs={{64,0},{128,64},{192,128},{256,192},{320,256},{384,320},{448,384},... | collective-permute-start | bytes 98312 | tf_op jit(solution)/shard_map/ppermute | solution.py:17
  171.1 12.3 %collective-permute-start.8 = (f32[64,128]{1,0:T(8,128)S(1)}, f32[64,128]{1,0:T(8,128)S(1)}, u32[]{:S(2)}, u32[]{:S(2)}) collective-permute-start(f32[64,128]{1,0:T(8,128)S(1)} %get-tuple-element.19), channel_id=1, source_target_pairs={{0,64},{64,128},{128,192},{192,256},{256,320},{320,384},{384,448},... | collective-permute-start | bytes 98312 | tf_op jit(solution)/shard_map/ppermute | solution.py:16
  173.0 10.4 %collective-permute-start.11 = (f32[64,128]{1,0:T(8,128)S(1)}, f32[64,128]{1,0:T(8,128)S(1)}, u32[]{:S(2)}, u32[]{:S(2)}) collective-permute-start(f32[64,128]{1,0:T(8,128)S(1)} %get-tuple-element.20), channel_id=1, source_target_pairs={{1,0},{2,1},{3,2},{4,3},{5,4},{6,5},{7,6},{8,7},{9,8},{10,9},{11,1... | collective-permute-start | bytes 98312 | tf_op jit(solution)/shard_map/ppermute | solution.py:19
  174.9 8.5 %collective-permute-start.10 = (f32[64,128]{1,0:T(8,128)S(1)}, f32[64,128]{1,0:T(8,128)S(1)}, u32[]{:S(2)}, u32[]{:S(2)}) collective-permute-start(f32[64,128]{1,0:T(8,128)S(1)} %get-tuple-element.21), channel_id=1, source_target_pairs={{0,1},{1,2},{2,3},{3,4},{4,5},{5,6},{6,7},{7,8},{8,9},{9,10},{10,1... | collective-permute-start | bytes 98312 | tf_op jit(solution)/shard_map/ppermute | solution.py:18
  180.4 6.2 %collective-permute-start.9 = (f32[64,128]{1,0:T(8,128)S(1)}, f32[64,128]{1,0:T(8,128)S(1)}, u32[]{:S(2)}, u32[]{:S(2)}) collective-permute-start(f32[64,128]{1,0:T(8,128)S(1)} %get-tuple-element.22), channel_id=1, source_target_pairs={{64,0},{128,64},{192,128},{256,192},{320,256},{384,320},{448,384},... | collective-permute-start | bytes 98312 | tf_op jit(solution)/shard_map/ppermute | solution.py:17
  243.1 23.1 %collective-permute-start.12 = (f32[64,128]{1,0:T(8,128)S(1)}, f32[64,128]{1,0:T(8,128)S(1)}, u32[]{:S(2)}, u32[]{:S(2)}) collective-permute-start(f32[64,128]{1,0:T(8,128)S(1)} %get-tuple-element.15), channel_id=1, source_target_pairs={{0,64},{64,128},{128,192},{192,256},{256,320},{320,384},{384,448},... | collective-permute-start | bytes 98312 | tf_op jit(solution)/shard_map/ppermute | solution.py:16
  256.5 9.7 %collective-permute-start.15 = (f32[64,128]{1,0:T(8,128)S(1)}, f32[64,128]{1,0:T(8,128)S(1)}, u32[]{:S(2)}, u32[]{:S(2)}) collective-permute-start(f32[64,128]{1,0:T(8,128)S(1)} %get-tuple-element.16), channel_id=1, source_target_pairs={{1,0},{2,1},{3,2},{4,3},{5,4},{6,5},{7,6},{8,7},{9,8},{10,9},{11,1... | collective-permute-start | bytes 98312 | tf_op jit(solution)/shard_map/ppermute | solution.py:19
  258.4 7.8 %collective-permute-start.14 = (f32[64,128]{1,0:T(8,128)S(1)}, f32[64,128]{1,0:T(8,128)S(1)}, u32[]{:S(2)}, u32[]{:S(2)}) collective-permute-start(f32[64,128]{1,0:T(8,128)S(1)} %get-tuple-element.17), channel_id=1, source_target_pairs={{0,1},{1,2},{2,3},{3,4},{4,5},{5,6},{6,7},{7,8},{8,9},{9,10},{10,1... | collective-permute-start | bytes 98312 | tf_op jit(solution)/shard_map/ppermute | solution.py:18
  263.9 5.2 %collective-permute-start.13 = (f32[64,128]{1,0:T(8,128)S(1)}, f32[64,128]{1,0:T(8,128)S(1)}, u32[]{:S(2)}, u32[]{:S(2)}) collective-permute-start(f32[64,128]{1,0:T(8,128)S(1)} %get-tuple-element.18), channel_id=1, source_target_pairs={{64,0},{128,64},{192,128},{256,192},{320,256},{384,320},{448,384},... | collective-permute-start | bytes 98312 | tf_op jit(solution)/shard_map/ppermute | solution.py:17
  270.1 12.5 %collective-permute-start.16 = (f32[64,128]{1,0:T(8,128)S(1)}, f32[64,128]{1,0:T(8,128)S(1)}, u32[]{:S(2)}, u32[]{:S(2)}) collective-permute-start(f32[64,128]{1,0:T(8,128)S(1)} %get-tuple-element.11), channel_id=1, source_target_pairs={{0,64},{64,128},{128,192},{192,256},{256,320},{320,384},{384,448},... | collective-permute-start | bytes 98312 | tf_op jit(solution)/shard_map/ppermute | solution.py:16
  272.0 10.6 %collective-permute-start.19 = (f32[64,128]{1,0:T(8,128)S(1)}, f32[64,128]{1,0:T(8,128)S(1)}, u32[]{:S(2)}, u32[]{:S(2)}) collective-permute-start(f32[64,128]{1,0:T(8,128)S(1)} %get-tuple-element.12), channel_id=1, source_target_pairs={{1,0},{2,1},{3,2},{4,3},{5,4},{6,5},{7,6},{8,7},{9,8},{10,9},{11,1... | collective-permute-start | bytes 98312 | tf_op jit(solution)/shard_map/ppermute | solution.py:19
  274.0 8.7 %collective-permute-start.18 = (f32[64,128]{1,0:T(8,128)S(1)}, f32[64,128]{1,0:T(8,128)S(1)}, u32[]{:S(2)}, u32[]{:S(2)}) collective-permute-start(f32[64,128]{1,0:T(8,128)S(1)} %get-tuple-element.13), channel_id=1, source_target_pairs={{0,1},{1,2},{2,3},{3,4},{4,5},{5,6},{6,7},{7,8},{8,9},{9,10},{10,1... | collective-permute-start | bytes 98312 | tf_op jit(solution)/shard_map/ppermute | solution.py:18
  279.6 6.0 %collective-permute-start.17 = (f32[64,128]{1,0:T(8,128)S(1)}, f32[64,128]{1,0:T(8,128)S(1)}, u32[]{:S(2)}, u32[]{:S(2)}) collective-permute-start(f32[64,128]{1,0:T(8,128)S(1)} %get-tuple-element.14), channel_id=1, source_target_pairs={{64,0},{128,64},{192,128},{256,192},{320,256},{384,320},{448,384},... | collective-permute-start | bytes 98312 | tf_op jit(solution)/shard_map/ppermute | solution.py:17
  344.2 22.6 %collective-permute-start.20 = (f32[64,128]{1,0:T(8,128)S(1)}, f32[64,128]{1,0:T(8,128)S(1)}, u32[]{:S(2)}, u32[]{:S(2)}) collective-permute-start(f32[64,128]{1,0:T(8,128)S(1)} %get-tuple-element.7), channel_id=1, source_target_pairs={{0,64},{64,128},{128,192},{192,256},{256,320},{320,384},{384,448},... | collective-permute-start | bytes 98312 | tf_op jit(solution)/shard_map/ppermute | solution.py:16
  357.1 9.7 %collective-permute-start.23 = (f32[64,128]{1,0:T(8,128)S(1)}, f32[64,128]{1,0:T(8,128)S(1)}, u32[]{:S(2)}, u32[]{:S(2)}) collective-permute-start(f32[64,128]{1,0:T(8,128)S(1)} %get-tuple-element.8), channel_id=1, source_target_pairs={{1,0},{2,1},{3,2},{4,3},{5,4},{6,5},{7,6},{8,7},{9,8},{10,9},{11,1... | collective-permute-start | bytes 98312 | tf_op jit(solution)/shard_map/ppermute | solution.py:19
  359.0 7.8 %collective-permute-start.22 = (f32[64,128]{1,0:T(8,128)S(1)}, f32[64,128]{1,0:T(8,128)S(1)}, u32[]{:S(2)}, u32[]{:S(2)}) collective-permute-start(f32[64,128]{1,0:T(8,128)S(1)} %get-tuple-element.9), channel_id=1, source_target_pairs={{0,1},{1,2},{2,3},{3,4},{4,5},{5,6},{6,7},{7,8},{8,9},{9,10},{10,1... | collective-permute-start | bytes 98312 | tf_op jit(solution)/shard_map/ppermute | solution.py:18
  364.5 5.2 %collective-permute-start.21 = (f32[64,128]{1,0:T(8,128)S(1)}, f32[64,128]{1,0:T(8,128)S(1)}, u32[]{:S(2)}, u32[]{:S(2)}) collective-permute-start(f32[64,128]{1,0:T(8,128)S(1)} %get-tuple-element.10), channel_id=1, source_target_pairs={{64,0},{128,64},{192,128},{256,192},{320,256},{384,320},{448,384},... | collective-permute-start | bytes 98312 | tf_op jit(solution)/shard_map/ppermute | solution.py:17

commit v2 on v1

--- a/solution.py
+++ b/solution.py
@@ -31,6 +31,12 @@
     return jnp.einsum("bf,jbn->fjn", selector_full, product, precision=HIGHEST)
 
 
+def gather(array, axis):
+    peers = lax.axis_size(axis)
+    copies = jnp.broadcast_to(array[None], (peers, *array.shape))
+    return lax.all_to_all(copies, axis, 0, 0, tiled=True)
+
+
 def in_three(array):
     high = lax.reduce_precision(array, 8, 7)
     rest = array - high
@@ -48,17 +54,17 @@
     return (high + middle) + low
 
 
-def own_inverse_rows(corner_ids, coarse_inverse):
-    peers = lax.axis_size("wide")
+def own_inverse_rows(corner_ids, ids, coarse_inverse):
+    peers, slots = ids.shape
     owned = coarse_inverse.shape[0]
-    prims = corner_ids.shape[0]
-    id_row = jnp.pad(corner_ids.astype(jnp.float32), (0, 128 - prims))[None, :]
-    ids = lax.all_gather(id_row, "wide")[:, 0, :prims].astype(jnp.int32).reshape(-1)
-    entries = pick_columns(coarse_inverse, ids)
-    entries = entries.reshape(owned, peers, prims).transpose(1, 2, 0).reshape(peers, prims * owned)
-    entries = lax.all_to_all(entries, "wide", 0, 0, tiled=True)
-    entries = entries.reshape(peers, prims, owned).transpose(1, 0, 2)
-    return entries.reshape(prims, peers * owned)
+    col = lax.axis_index("wide")
+    entries = pick_columns(coarse_inverse, ids.reshape(-1))
+    entries = entries.reshape(owned, peers, slots).transpose(1, 0, 2)
+    entries = lax.all_to_all(entries.reshape(peers, owned * slots), "wide", 0, 0, tiled=True)
+    entries = entries.reshape(peers * owned, slots)
+    column_ids = lax.dynamic_index_in_dim(ids, col, 0, keepdims=False)
+    mine = (corner_ids[:, None] == column_ids[None, :]).astype(jnp.float32)
+    return jnp.einsum("ps,ks->pk", mine, entries, precision=HIGHEST)
 
 
 def slots_of_column(ids, amount):
@@ -98,7 +104,6 @@
     inner = jnp.stack([row > 0, row < rows_total - 1, col > 0, col < cols_total - 1])
     weights = jnp.where(inner, jnp.float32(0.5), jnp.float32(1.0))[:, None, None]
     basis = coarse_basis.astype(jnp.float32)
-    inverse_rows = own_inverse_rows(corner_ids, coarse_inverse)
     id_lanes = jnp.broadcast_to(corner_ids.astype(jnp.float32)[:, None], (prims, rhs))
     solution = jnp.zeros(load_faces.shape, jnp.float32)
     for iteration in range(ITERS):
@@ -110,24 +115,24 @@
             )
         weighted = weights * residual
         restricted = jnp.einsum("pfn,fjn->pj", basis, weighted, precision=HIGHEST)
-        in_column = lax.all_gather(
-            jnp.concatenate([restricted, id_lanes], axis=1), "sub", axis=0, tiled=True
-        )
+        in_column = gather(jnp.concatenate([restricted, id_lanes], axis=1), "sub")
+        in_column = in_column.reshape(rows_total * prims, 2 * rhs)
         if iteration == 0:
             slots, slot_ids = slots_of_column(in_column[:, rhs], 2 * half_slots)
         summed = jnp.dot(slots, in_column[:, :rhs], precision=HIGHEST)
         summed = jnp.concatenate([summed[:half_slots], summed[half_slots:]], axis=1)
         if iteration == 0:
             id_row = jnp.pad(slot_ids, (0, 2 * rhs - 2 * half_slots))[None, :]
-            everyone = lax.all_gather(jnp.concatenate([summed, id_row]), "wide")
+            everyone = gather(jnp.concatenate([summed, id_row]), "wide")
             ids = everyone[:, half_slots, : 2 * half_slots].astype(jnp.int32)
             everyone = everyone[:, :half_slots]
+            inverse_rows = own_inverse_rows(corner_ids, ids, coarse_inverse)
             ids = ids.reshape(cols_total, 2, half_slots).transpose(1, 0, 2).reshape(-1)
             rows_at = pick_columns(inverse_rows, ids)
             rows_at = rows_at.reshape(prims, 2, cols_total * half_slots)
             rows_at = rows_at.transpose(1, 0, 2).reshape(2 * prims, -1)
         else:
-            everyone = lax.all_gather(summed, "wide")
+            everyone = gather(summed, "wide")
         solved = jnp.dot(
             rows_at, everyone.reshape(cols_total * half_slots, 2 * rhs), precision=HIGHEST
         )

time: 372 us -> 277 us (0.74)
  blocking collectives: 222 us -> 23.6 us
  waiting for transfers between devices: 13.6 us -> 96.5 us
  starting transfers between devices: 116 us -> 129 us
  local copies, waits for them, and re-layouts: 3.61 us -> 8.31 us
    all_gather x7 -> x0, blocking collectives: 222 us -> none  [the longest x2 78.8 us: body(): everyone = lax.all_gather(summed, 'wide')]
    all_to_all x1 -> x5, waiting for transfers between devices: 0.01 us -> 80 us  [the longest x4 71.4 us: gather(): return lax.all_to_all(copies, axis, 0, 0, tiled=True)]
    all_to_all x1 -> x5, starting transfers between devices: 8.15 us -> 48.8 us  [the longest x4 41.5 us: gather(): return lax.all_to_all(copies, axis, 0, 0, tiled=True)]
    ppermute x6, starting transfers between devices: 47.6 us -> 22.5 us  [assemble(): from_north = lax.ppermute(faces[1], 'sub', down)]
    all_to_all x0 -> x2, blocking collectives: none -> 23.6 us  [gather(): return lax.all_to_all(copies, axis, 0, 0, tiled=True)]
  transfers between devices with their start and end apart: 25 -> 29, of which waited for: 5 -> 11; matrix products, arithmetic and copies ran while one was open for 2% -> 2% of each run, Pallas kernels for 0% -> 0%
where the time goes in v2:
time: 277 us; the launch traced here: 275 us
  starting transfers between devices  129 us (47%)
  waiting for transfers between devices  96.5 us (35%)
  blocking collectives  23.6 us (9%)
  matrix products  13.2 us (5%)
  local copies, waits for them, and re-layouts  8.31 us (3%)
  other arithmetic  3.55 us (1%)
    all_to_all x4, waiting for transfers between devices, gather(): return lax.all_to_all(copies, axis, 0, 0, tiled=True)  71.4 us
    all_to_all x4, starting transfers between devices, gather(): return lax.all_to_all(copies, axis, 0, 0, tiled=True)  41.5 us
    ppermute x6, starting transfers between devices, assemble(): from_west = lax.ppermute(faces[3], 'wide', right)  31.2 us
    all_to_all x2, blocking collectives, gather(): return lax.all_to_all(copies, axis, 0, 0, tiled=True)  23.6 us
    ppermute x6, starting transfers between devices, assemble(): from_north = lax.ppermute(faces[1], 'sub', down)  22.5 us
    ppermute x6, waiting for transfers between devices, assemble(): from_south = lax.ppermute(faces[0], 'sub', [(b, a) for a, b in down])  16.4 us
    ppermute x6, starting transfers between devices, assemble(): from_south = lax.ppermute(faces[0], 'sub', [(b, a) for a, b in down])  13.8 us
    ppermute x6, starting transfers between devices, assemble(): from_east = lax.ppermute(faces[2], 'wide', [(b, a) for a, b in right])  13.2 us
  transfers between devices with their start and end apart: 29, of which 11 were waited for; matrix products, arithmetic and copies ran while one was open for 2% of the time, Pallas kernels for 0%

profile of v2, /device:TPU:15, one launch (start us, length us, event | category | flops | bytes accessed | tf_op | source)
XLA Modules:
  0.0 275.4 jit_solution(317165674337514266)
XLA Ops:
  0.0 0.7 copy-done
  0.7 0.9 convolution_bitcast_fusion.3
  1.6 5.5 %collective-permute-start = (f32[64,128]{1,0:T(8,128)S(1)}, f32[64,128]{1,0:T(8,128)S(1)}, u32[]{:S(2)}, u32[]{:S(2)}) collective-permute-start(f32[64,128]{1,0:T(8,128)S(1)} %get-tuple-element.27), channel_id=1, source_target_pairs={{0,64},{64,128},{128,192},{192,256},{256,320},{320,384},{384,448},... | collective-permute-start | bytes 98312 | tf_op jit(solution)/shard_map/ppermute | solution.py:16
  7.1 3.1 %collective-permute-start.3 = (f32[64,128]{1,0:T(8,128)S(1)}, f32[64,128]{1,0:T(8,128)S(1)}, u32[]{:S(2)}, u32[]{:S(2)}) collective-permute-start(f32[64,128]{1,0:T(8,128)S(1)} %get-tuple-element.28), channel_id=1, source_target_pairs={{1,0},{2,1},{3,2},{4,3},{5,4},{6,5},{7,6},{8,7},{9,8},{10,9},{11,1... | collective-permute-start | bytes 98312 | tf_op jit(solution)/shard_map/ppermute | solution.py:19
  10.1 4.3 %collective-permute-start.2 = (f32[64,128]{1,0:T(8,128)S(1)}, f32[64,128]{1,0:T(8,128)S(1)}, u32[]{:S(2)}, u32[]{:S(2)}) collective-permute-start(f32[64,128]{1,0:T(8,128)S(1)} %get-tuple-element.29), channel_id=1, source_target_pairs={{0,1},{1,2},{2,3},{3,4},{4,5},{5,6},{6,7},{7,8},{8,9},{9,10},{10,1... | collective-permute-start | bytes 98312 | tf_op jit(solution)/shard_map/ppermute | solution.py:18
  14.5 1.9 collective-permute-start.1
  16.4 0.7 bitcast_convert_fusion
  17.2 2.5 collective-permute-done.1
  19.7 0.9 convolution_bitcast_fusion.6
  20.8 0.7 broadcast_in_dim.53
  21.4 15.0 %all-to-all-start = ((f32[16,4,128]{2,1,0:T(4,128)}), f32[16,4,128]{2,1,0:T(4,128)S(1)}, u32[]{:S(2)}, u32[]{:S(2)}) async-start(f32[16,4,128]{2,1,0:T(4,128)} %broadcast_in_dim.53), calls=%async_computation | async-start | bytes 65536 | tf_op jit(solution)/shard_map/all_to_all | solution.py:37
  36.6 7.2 %all-to-all-done = f32[16,4,128]{2,1,0:T(4,128)S(1)} async-done(((f32[16,4,128]{2,1,0:T(4,128)}), f32[16,4,128]{2,1,0:T(4,128)S(1)}, u32[]{:S(2)}, u32[]{:S(2)}) %all-to-all-start) | async-done | bytes 32800 | tf_op jit(solution)/shard_map/all_to_all | solution.py:37
  44.9 1.0 broadcast_in_dim.59
  45.8 10.9 %all-to-all-start.1 = ((f32[64,18,128]{2,1,0:T(8,128)}), f32[64,18,128]{2,1,0:T(8,128)S(1)}, u32[]{:S(2)}, u32[]{:S(2)}) async-start(f32[64,18,128]{2,1,0:T(8,128)} %broadcast_in_dim.59), calls=%async_computation.1 | async-start | bytes 1572864 | tf_op jit(solution)/shard_map/all_to_all | solution.py:37
  57.7 21.4 %all-to-all-done.1 = f32[64,18,128]{2,1,0:T(8,128)S(1)} async-done(((f32[64,18,128]{2,1,0:T(8,128)}), f32[64,18,128]{2,1,0:T(8,128)S(1)}, u32[]{:S(2)}, u32[]{:S(2)}) %all-to-all-start.1) | async-done | bytes 589856 | tf_op jit(solution)/shard_map/all_to_all | solution.py:37
  79.3 2.0 fusion
  81.4 0.7 reshape.128
  82.4 0.8 copy.140
  83.2 7.3 %all-to-all-start.2 = ((f32[64,1,612]{2,1,0:T(1,128)}), f32[64,1,612]{2,1,0:T(1,128)S(1)}, u32[]{:S(2)}, u32[]{:S(2)}) async-start(f32[64,1,612]{2,1,0:T(1,128)} %copy.140), calls=%async_computation.2 | async-start | bytes 327680 | tf_op jit(solution)/shard_map/all_to_all | solution.py:63
  91.1 8.7 %all-to-all-done.2 = f32[64,1,612]{2,1,0:T(1,128)S(1)} async-done(((f32[64,1,612]{2,1,0:T(1,128)}), f32[64,1,612]{2,1,0:T(1,128)S(1)}, u32[]{:S(2)}, u32[]{:S(2)}) %all-to-all-start.2) | async-done | bytes 156704 | tf_op jit(solution)/shard_map/all_to_all | solution.py:63
  99.8 0.4 reduce.2
  100.2 0.4 reshape.129
  100.5 0.4 reduce-precision_convert_fusion.3
  101.0 1.8 fusion.1
  103.0 0.4 fusion.123
  103.5 0.3 fusion.5
  103.9 5.0 %collective-permute-start.4 = (f32[64,128]{1,0:T(8,128)S(1)}, f32[64,128]{1,0:T(8,128)S(1)}, u32[]{:S(2)}, u32[]{:S(2)}) collective-permute-start(f32[64,128]{1,0:T(8,128)S(1)} %get-tuple-element.23), channel_id=1, source_target_pairs={{0,64},{64,128},{128,192},{192,256},{256,320},{320,384},{384,448},... | collective-permute-start | bytes 98312 | tf_op jit(solution)/shard_map/ppermute | solution.py:16
  108.9 2.1 collective-permute-start.7
  111.0 5.3 %collective-permute-start.6 = (f32[64,128]{1,0:T(8,128)S(1)}, f32[64,128]{1,0:T(8,128)S(1)}, u32[]{:S(2)}, u32[]{:S(2)}) collective-permute-start(f32[64,128]{1,0:T(8,128)S(1)} %get-tuple-element.25), channel_id=1, source_target_pairs={{0,1},{1,2},{2,3},{3,4},{4,5},{5,6},{6,7},{7,8},{8,9},{9,10},{10,1... | collective-permute-start | bytes 98312 | tf_op jit(solution)/shard_map/ppermute | solution.py:18
  116.3 1.9 collective-permute-start.5
  118.5 3.0 %collective-permute-done.5 = f32[64,128]{1,0:T(8,128)S(1)} collective-permute-done((f32[64,128]{1,0:T(8,128)S(1)}, f32[64,128]{1,0:T(8,128)S(1)}, u32[]{:S(2)}, u32[]{:S(2)}) %collective-permute-start.5) | collective-permute-done | bytes 32800 | tf_op jit(solution)/shard_map/ppermute | solution.py:17
  122.5 1.9 collective-permute-start.8
  124.4 1.9 collective-permute-start.11
  126.3 5.5 %collective-permute-start.10 = (f32[64,128]{1,0:T(8,128)S(1)}, f32[64,128]{1,0:T(8,128)S(1)}, u32[]{:S(2)}, u32[]{:S(2)}) collective-permute-start(f32[64,128]{1,0:T(8,128)S(1)} %get-tuple-element.21), channel_id=1, source_target_pairs={{0,1},{1,2},{2,3},{3,4},{4,5},{5,6},{6,7},{7,8},{8,9},{9,10},{10,1... | collective-permute-start | bytes 98312 | tf_op jit(solution)/shard_map/ppermute | solution.py:18
  131.8 3.1 %collective-permute-start.9 = (f32[64,128]{1,0:T(8,128)S(1)}, f32[64,128]{1,0:T(8,128)S(1)}, u32[]{:S(2)}, u32[]{:S(2)}) collective-permute-start(f32[64,128]{1,0:T(8,128)S(1)} %get-tuple-element.22), channel_id=1, source_target_pairs={{64,0},{128,64},{192,128},{256,192},{320,256},{384,320},{448,384},... | collective-permute-start | bytes 98312 | tf_op jit(solution)/shard_map/ppermute | solution.py:17
  135.0 2.0 collective-permute-done.9
  137.4 11.8 %all_to_all.39 = f32[16,4,128]{2,1,0:T(4,128)S(1)} all-to-all(f32[16,4,128]{2,1,0:T(4,128)S(1)} %broadcast_in_dim.60), channel_id=1, replica_groups=mesh['sub'=16,'wide'=64] {'sub'}, dimensions={0} | all-to-all | bytes 65536 | tf_op jit(solution)/shard_map/all_to_all | solution.py:37
  149.4 1.0 broadcast_in_dim.61
  150.4 8.2 %all-to-all-start.4 = ((f32[64,17,128]{2,1,0:T(8,128)}), f32[64,17,128]{2,1,0:T(8,128)S(1)}, u32[]{:S(2)}, u32[]{:S(2)}) async-start(f32[64,17,128]{2,1,0:T(8,128)} %broadcast_in_dim.61), calls=%async_computation.4 | async-start | bytes 1572864 | tf_op jit(solution)/shard_map/all_to_all | solution.py:37
  159.5 21.4 %all-to-all-done.4 = f32[64,17,128]{2,1,0:T(8,128)S(1)} async-done(((f32[64,17,128]{2,1,0:T(8,128)}), f32[64,17,128]{2,1,0:T(8,128)S(1)}, u32[]{:S(2)}, u32[]{:S(2)}) %all-to-all-start.4) | async-done | bytes 557088 | tf_op jit(solution)/shard_map/all_to_all | solution.py:37
  181.0 0.4 fusion.126
  181.4 0.4 fusion.7
  181.7 4.1 %collective-permute-start.12 = (f32[64,128]{1,0:T(8,128)S(1)}, f32[64,128]{1,0:T(8,128)S(1)}, u32[]{:S(2)}, u32[]{:S(2)}) collective-permute-start(f32[64,128]{1,0:T(8,128)S(1)} %get-tuple-element.15), channel_id=1, source_target_pairs={{0,64},{64,128},{128,192},{192,256},{256,320},{320,384},{384,448},... | collective-permute-start | bytes 98312 | tf_op jit(solution)/shard_map/ppermute | solution.py:16
  185.8 2.1 collective-permute-start.15
  187.9 5.3 %collective-permute-start.14 = (f32[64,128]{1,0:T(8,128)S(1)}, f32[64,128]{1,0:T(8,128)S(1)}, u32[]{:S(2)}, u32[]{:S(2)}) collective-permute-start(f32[64,128]{1,0:T(8,128)S(1)} %get-tuple-element.17), channel_id=1, source_target_pairs={{0,1},{1,2},{2,3},{3,4},{4,5},{5,6},{6,7},{7,8},{8,9},{9,10},{10,1... | collective-permute-start | bytes 98312 | tf_op jit(solution)/shard_map/ppermute | solution.py:18
  193.2 1.9 collective-permute-start.13
  195.2 3.3 %collective-permute-done.13 = f32[64,128]{1,0:T(8,128)S(1)} collective-permute-done((f32[64,128]{1,0:T(8,128)S(1)}, f32[64,128]{1,0:T(8,128)S(1)}, u32[]{:S(2)}, u32[]{:S(2)}) %collective-permute-start.13) | collective-permute-done | bytes 32800 | tf_op jit(solution)/shard_map/ppermute | solution.py:17
  199.5 1.9 collective-permute-start.16
  201.4 1.9 collective-permute-start.19
  203.3 5.5 %collective-permute-start.18 = (f32[64,128]{1,0:T(8,128)S(1)}, f32[64,128]{1,0:T(8,128)S(1)}, u32[]{:S(2)}, u32[]{:S(2)}) collective-permute-start(f32[64,128]{1,0:T(8,128)S(1)} %get-tuple-element.13), channel_id=1, source_target_pairs={{0,1},{1,2},{2,3},{3,4},{4,5},{5,6},{6,7},{7,8},{8,9},{9,10},{10,1... | collective-permute-start | bytes 98312 | tf_op jit(solution)/shard_map/ppermute | solution.py:18
  208.8 3.0 %collective-permute-start.17 = (f32[64,128]{1,0:T(8,128)S(1)}, f32[64,128]{1,0:T(8,128)S(1)}, u32[]{:S(2)}, u32[]{:S(2)}) collective-permute-start(f32[64,128]{1,0:T(8,128)S(1)} %get-tuple-element.14), channel_id=1, source_target_pairs={{64,0},{128,64},{192,128},{256,192},{320,256},{384,320},{448,384},... | collective-permute-start | bytes 98312 | tf_op jit(solution)/shard_map/ppermute | solution.py:17
  211.8 2.2 collective-permute-done.17
  214.4 11.8 %all_to_all.40 = f32[16,4,128]{2,1,0:T(4,128)S(1)} all-to-all(f32[16,4,128]{2,1,0:T(4,128)S(1)} %broadcast_in_dim.62), channel_id=1, replica_groups=mesh['sub'=16,'wide'=64] {'sub'}, dimensions={0} | all-to-all | bytes 65536 | tf_op jit(solution)/shard_map/all_to_all | solution.py:37
  226.4 1.0 broadcast_in_dim.63
  227.4 7.5 %all-to-all-start.6 = ((f32[64,17,128]{2,1,0:T(8,128)}), f32[64,17,128]{2,1,0:T(8,128)S(1)}, u32[]{:S(2)}, u32[]{:S(2)}) async-start(f32[64,17,128]{2,1,0:T(8,128)} %broadcast_in_dim.63), calls=%async_computation.6 | async-start | bytes 1572864 | tf_op jit(solution)/shard_map/all_to_all | solution.py:37
  235.8 21.4 %all-to-all-done.6 = f32[64,17,128]{2,1,0:T(8,128)S(1)} async-done(((f32[64,17,128]{2,1,0:T(8,128)}), f32[64,17,128]{2,1,0:T(8,128)S(1)}, u32[]{:S(2)}, u32[]{:S(2)}) %all-to-all-start.6) | async-done | bytes 557088 | tf_op jit(solution)/shard_map/all_to_all | solution.py:37
  257.3 0.4 fusion.129
  257.6 0.4 fusion.9
  258.0 4.1 %collective-permute-start.20 = (f32[64,128]{1,0:T(8,128)S(1)}, f32[64,128]{1,0:T(8,128)S(1)}, u32[]{:S(2)}, u32[]{:S(2)}) collective-permute-start(f32[64,128]{1,0:T(8,128)S(1)} %get-tuple-element.7), channel_id=1, source_target_pairs={{0,64},{64,128},{128,192},{192,256},{256,320},{320,384},{384,448},... | collective-permute-start | bytes 98312 | tf_op jit(solution)/shard_map/ppermute | solution.py:16
  262.1 2.1 collective-permute-start.23
  264.2 5.3 %collective-permute-start.22 = (f32[64,128]{1,0:T(8,128)S(1)}, f32[64,128]{1,0:T(8,128)S(1)}, u32[]{:S(2)}, u32[]{:S(2)}) collective-permute-start(f32[64,128]{1,0:T(8,128)S(1)} %get-tuple-element.9), channel_id=1, source_target_pairs={{0,1},{1,2},{2,3},{3,4},{4,5},{5,6},{6,7},{7,8},{8,9},{9,10},{10,1... | collective-permute-start | bytes 98312 | tf_op jit(solution)/shard_map/ppermute | solution.py:18
  269.5 1.9 collective-permute-start.21
  271.5 3.3 %collective-permute-done.21 = f32[64,128]{1,0:T(8,128)S(1)} collective-permute-done((f32[64,128]{1,0:T(8,128)S(1)}, f32[64,128]{1,0:T(8,128)S(1)}, u32[]{:S(2)}, u32[]{:S(2)}) %collective-permute-start.21) | collective-permute-done | bytes 32800 | tf_op jit(solution)/shard_map/ppermute | solution.py:17
  274.7 0.7 fusion.23
  (110 shorter events, 9.1 us)
Async XLA Ops:
  0.0 0.7 copy-start
  0.0 36.4 %copy-start.1 = (bf16[1,1,512,512]{3,2,1,0:T(8,128)(2,1)S(1)}, bf16[1,1,512,512]{3,2,1,0:T(8,128)(2,1)}, u32[]{:S(2)}) copy-start(bf16[1,1,512,512]{3,2,1,0:T(8,128)(2,1)} %param.12) | copy-start | bytes 1572868
  1.6 15.6 %collective-permute-start = (f32[64,128]{1,0:T(8,128)S(1)}, f32[64,128]{1,0:T(8,128)S(1)}, u32[]{:S(2)}, u32[]{:S(2)}) collective-permute-start(f32[64,128]{1,0:T(8,128)S(1)} %get-tuple-element.27), channel_id=1, source_target_pairs={{0,64},{64,128},{128,192},{192,256},{256,320},{320,384},{384,448},... | collective-permute-start | bytes 98312 | tf_op jit(solution)/shard_map/ppermute | solution.py:16
  7.1 10.1 %collective-permute-start.3 = (f32[64,128]{1,0:T(8,128)S(1)}, f32[64,128]{1,0:T(8,128)S(1)}, u32[]{:S(2)}, u32[]{:S(2)}) collective-permute-start(f32[64,128]{1,0:T(8,128)S(1)} %get-tuple-element.28), channel_id=1, source_target_pairs={{1,0},{2,1},{3,2},{4,3},{5,4},{6,5},{7,6},{8,7},{9,8},{10,9},{11,1... | collective-permute-start | bytes 98312 | tf_op jit(solution)/shard_map/ppermute | solution.py:19
  10.1 7.0 %collective-permute-start.2 = (f32[64,128]{1,0:T(8,128)S(1)}, f32[64,128]{1,0:T(8,128)S(1)}, u32[]{:S(2)}, u32[]{:S(2)}) collective-permute-start(f32[64,128]{1,0:T(8,128)S(1)} %get-tuple-element.29), channel_id=1, source_target_pairs={{0,1},{1,2},{2,3},{3,4},{4,5},{5,6},{6,7},{7,8},{8,9},{9,10},{10,1... | collective-permute-start | bytes 98312 | tf_op jit(solution)/shard_map/ppermute | solution.py:18
  14.5 5.2 %collective-permute-start.1 = (f32[64,128]{1,0:T(8,128)S(1)}, f32[64,128]{1,0:T(8,128)S(1)}, u32[]{:S(2)}, u32[]{:S(2)}) collective-permute-start(f32[64,128]{1,0:T(8,128)S(1)} %get-tuple-element.30), channel_id=1, source_target_pairs={{64,0},{128,64},{192,128},{256,192},{320,256},{384,320},{448,384},... | collective-permute-start | bytes 98312 | tf_op jit(solution)/shard_map/ppermute | solution.py:17
  21.4 22.4 %all-to-all-start = ((f32[16,4,128]{2,1,0:T(4,128)}), f32[16,4,128]{2,1,0:T(4,128)S(1)}, u32[]{:S(2)}, u32[]{:S(2)}) async-start(f32[16,4,128]{2,1,0:T(4,128)} %broadcast_in_dim.53), calls=%async_computation | async-start | bytes 65536 | tf_op jit(solution)/shard_map/all_to_all | solution.py:37
  45.8 10.9 %copy-start.3 = (f32[18,1152]{1,0:T(8,128)S(1)}, f32[18,1152]{1,0:T(8,128)}, u32[]{:S(2)}) copy-start(f32[18,1152]{1,0:T(8,128)} %param.15) | copy-start | bytes 248836
  45.8 11.0 %copy-start.5 = (s32[1,1,4]{2,1,0:T(1,128)S(1)}, s32[1,1,4]{2,1,0:T(1,128)}, u32[]{:S(2)}) copy-start(s32[1,1,4]{2,1,0:T(1,128)} %param.10) | copy-start | bytes 52
  45.8 33.3 %all-to-all-start.1 = ((f32[64,18,128]{2,1,0:T(8,128)}), f32[64,18,128]{2,1,0:T(8,128)S(1)}, u32[]{:S(2)}, u32[]{:S(2)}) async-start(f32[64,18,128]{2,1,0:T(8,128)} %broadcast_in_dim.59), calls=%async_computation.1 | async-start | bytes 1572864 | tf_op jit(solution)/shard_map/all_to_all | solution.py:37
  83.2 16.5 %all-to-all-start.2 = ((f32[64,1,612]{2,1,0:T(1,128)}), f32[64,1,612]{2,1,0:T(1,128)S(1)}, u32[]{:S(2)}, u32[]{:S(2)}) async-start(f32[64,1,612]{2,1,0:T(1,128)} %copy.140), calls=%async_computation.2 | async-start | bytes 327680 | tf_op jit(solution)/shard_map/all_to_all | solution.py:63
  91.1 9.4 %copy-start.6 = (s32[1,1,4]{2,1,0:T(1,128)S(1)}, s32[1,1,4]{2,1,0:T(1,128)}, u32[]{:S(2)}) copy-start(s32[1,1,4]{2,1,0:T(1,128)} %param.14) | copy-start | bytes 52
  102.8 0.7 copy-start.4
  102.8 15.4 %copy-start.2 = (bf16[1,1,512,512]{3,2,1,0:T(8,128)(2,1)S(1)}, bf16[1,1,512,512]{3,2,1,0:T(8,128)(2,1)}, u32[]{:S(2)}) copy-start(bf16[1,1,512,512]{3,2,1,0:T(8,128)(2,1)} %param.11) | copy-start | bytes 1572868
  103.9 14.6 %collective-permute-start.4 = (f32[64,128]{1,0:T(8,128)S(1)}, f32[64,128]{1,0:T(8,128)S(1)}, u32[]{:S(2)}, u32[]{:S(2)}) collective-permute-start(f32[64,128]{1,0:T(8,128)S(1)} %get-tuple-element.23), channel_id=1, source_target_pairs={{0,64},{64,128},{128,192},{192,256},{256,320},{320,384},{384,448},... | collective-permute-start | bytes 98312 | tf_op jit(solution)/shard_map/ppermute | solution.py:16
  108.9 9.6 %collective-permute-start.7 = (f32[64,128]{1,0:T(8,128)S(1)}, f32[64,128]{1,0:T(8,128)S(1)}, u32[]{:S(2)}, u32[]{:S(2)}) collective-permute-start(f32[64,128]{1,0:T(8,128)S(1)} %get-tuple-element.24), channel_id=1, source_target_pairs={{1,0},{2,1},{3,2},{4,3},{5,4},{6,5},{7,6},{8,7},{9,8},{10,9},{11,1... | collective-permute-start | bytes 98312 | tf_op jit(solution)/shard_map/ppermute | solution.py:19
  111.0 7.5 %collective-permute-start.6 = (f32[64,128]{1,0:T(8,128)S(1)}, f32[64,128]{1,0:T(8,128)S(1)}, u32[]{:S(2)}, u32[]{:S(2)}) collective-permute-start(f32[64,128]{1,0:T(8,128)S(1)} %get-tuple-element.25), channel_id=1, source_target_pairs={{0,1},{1,2},{2,3},{3,4},{4,5},{5,6},{6,7},{7,8},{8,9},{9,10},{10,1... | collective-permute-start | bytes 98312 | tf_op jit(solution)/shard_map/ppermute | solution.py:18
  116.3 5.2 %collective-permute-start.5 = (f32[64,128]{1,0:T(8,128)S(1)}, f32[64,128]{1,0:T(8,128)S(1)}, u32[]{:S(2)}, u32[]{:S(2)}) collective-permute-start(f32[64,128]{1,0:T(8,128)S(1)} %get-tuple-element.26), channel_id=1, source_target_pairs={{64,0},{128,64},{192,128},{256,192},{320,256},{384,320},{448,384},... | collective-permute-start | bytes 98312 | tf_op jit(solution)/shard_map/ppermute | solution.py:17
  122.5 12.5 %collective-permute-start.8 = (f32[64,128]{1,0:T(8,128)S(1)}, f32[64,128]{1,0:T(8,128)S(1)}, u32[]{:S(2)}, u32[]{:S(2)}) collective-permute-start(f32[64,128]{1,0:T(8,128)S(1)} %get-tuple-element.19), channel_id=1, source_target_pairs={{0,64},{64,128},{128,192},{192,256},{256,320},{320,384},{384,448},... | collective-permute-start | bytes 98312 | tf_op jit(solution)/shard_map/ppermute | solution.py:16
  124.4 10.6 %collective-permute-start.11 = (f32[64,128]{1,0:T(8,128)S(1)}, f32[64,128]{1,0:T(8,128)S(1)}, u32[]{:S(2)}, u32[]{:S(2)}) collective-permute-start(f32[64,128]{1,0:T(8,128)S(1)} %get-tuple-element.20), channel_id=1, source_target_pairs={{1,0},{2,1},{3,2},{4,3},{5,4},{6,5},{7,6},{8,7},{9,8},{10,9},{11,1... | collective-permute-start | bytes 98312 | tf_op jit(solution)/shard_map/ppermute | solution.py:19
  126.3 8.7 %collective-permute-start.10 = (f32[64,128]{1,0:T(8,128)S(1)}, f32[64,128]{1,0:T(8,128)S(1)}, u32[]{:S(2)}, u32[]{:S(2)}) collective-permute-start(f32[64,128]{1,0:T(8,128)S(1)} %get-tuple-element.21), channel_id=1, source_target_pairs={{0,1},{1,2},{2,3},{3,4},{4,5},{5,6},{6,7},{7,8},{8,9},{9,10},{10,1... | collective-permute-start | bytes 98312 | tf_op jit(solution)/shard_map/ppermute | solution.py:18
  131.8 5.2 %collective-permute-start.9 = (f32[64,128]{1,0:T(8,128)S(1)}, f32[64,128]{1,0:T(8,128)S(1)}, u32[]{:S(2)}, u32[]{:S(2)}) collective-permute-start(f32[64,128]{1,0:T(8,128)S(1)} %get-tuple-element.22), channel_id=1, source_target_pairs={{64,0},{128,64},{192,128},{256,192},{320,256},{384,320},{448,384},... | collective-permute-start | bytes 98312 | tf_op jit(solution)/shard_map/ppermute | solution.py:17
  150.4 30.6 %all-to-all-start.4 = ((f32[64,17,128]{2,1,0:T(8,128)}), f32[64,17,128]{2,1,0:T(8,128)S(1)}, u32[]{:S(2)}, u32[]{:S(2)}) async-start(f32[64,17,128]{2,1,0:T(8,128)} %broadcast_in_dim.61), calls=%async_computation.4 | async-start | bytes 1572864 | tf_op jit(solution)/shard_map/all_to_all | solution.py:37
  181.7 13.4 %collective-permute-start.12 = (f32[64,128]{1,0:T(8,128)S(1)}, f32[64,128]{1,0:T(8,128)S(1)}, u32[]{:S(2)}, u32[]{:S(2)}) collective-permute-start(f32[64,128]{1,0:T(8,128)S(1)} %get-tuple-element.15), channel_id=1, source_target_pairs={{0,64},{64,128},{128,192},{192,256},{256,320},{320,384},{384,448},... | collective-permute-start | bytes 98312 | tf_op jit(solution)/shard_map/ppermute | solution.py:16
  185.8 9.3 %collective-permute-start.15 = (f32[64,128]{1,0:T(8,128)S(1)}, f32[64,128]{1,0:T(8,128)S(1)}, u32[]{:S(2)}, u32[]{:S(2)}) collective-permute-start(f32[64,128]{1,0:T(8,128)S(1)} %get-tuple-element.16), channel_id=1, source_target_pairs={{1,0},{2,1},{3,2},{4,3},{5,4},{6,5},{7,6},{8,7},{9,8},{10,9},{11,1... | collective-permute-start | bytes 98312 | tf_op jit(solution)/shard_map/ppermute | solution.py:19
  187.9 7.2 %collective-permute-start.14 = (f32[64,128]{1,0:T(8,128)S(1)}, f32[64,128]{1,0:T(8,128)S(1)}, u32[]{:S(2)}, u32[]{:S(2)}) collective-permute-start(f32[64,128]{1,0:T(8,128)S(1)} %get-tuple-element.17), channel_id=1, source_target_pairs={{0,1},{1,2},{2,3},{3,4},{4,5},{5,6},{6,7},{7,8},{8,9},{9,10},{10,1... | collective-permute-start | bytes 98312 | tf_op jit(solution)/shard_map/ppermute | solution.py:18
  193.2 5.2 %collective-permute-start.13 = (f32[64,128]{1,0:T(8,128)S(1)}, f32[64,128]{1,0:T(8,128)S(1)}, u32[]{:S(2)}, u32[]{:S(2)}) collective-permute-start(f32[64,128]{1,0:T(8,128)S(1)} %get-tuple-element.18), channel_id=1, source_target_pairs={{64,0},{128,64},{192,128},{256,192},{320,256},{384,320},{448,384},... | collective-permute-start | bytes 98312 | tf_op jit(solution)/shard_map/ppermute | solution.py:17
  199.5 12.3 %collective-permute-start.16 = (f32[64,128]{1,0:T(8,128)S(1)}, f32[64,128]{1,0:T(8,128)S(1)}, u32[]{:S(2)}, u32[]{:S(2)}) collective-permute-start(f32[64,128]{1,0:T(8,128)S(1)} %get-tuple-element.11), channel_id=1, source_target_pairs={{0,64},{64,128},{128,192},{192,256},{256,320},{320,384},{384,448},... | collective-permute-start | bytes 98312 | tf_op jit(solution)/shard_map/ppermute | solution.py:16
  201.4 10.4 %collective-permute-start.19 = (f32[64,128]{1,0:T(8,128)S(1)}, f32[64,128]{1,0:T(8,128)S(1)}, u32[]{:S(2)}, u32[]{:S(2)}) collective-permute-start(f32[64,128]{1,0:T(8,128)S(1)} %get-tuple-element.12), channel_id=1, source_target_pairs={{1,0},{2,1},{3,2},{4,3},{5,4},{6,5},{7,6},{8,7},{9,8},{10,9},{11,1... | collective-permute-start | bytes 98312 | tf_op jit(solution)/shard_map/ppermute | solution.py:19
  203.3 8.5 %collective-permute-start.18 = (f32[64,128]{1,0:T(8,128)S(1)}, f32[64,128]{1,0:T(8,128)S(1)}, u32[]{:S(2)}, u32[]{:S(2)}) collective-permute-start(f32[64,128]{1,0:T(8,128)S(1)} %get-tuple-element.13), channel_id=1, source_target_pairs={{0,1},{1,2},{2,3},{3,4},{4,5},{5,6},{6,7},{7,8},{8,9},{9,10},{10,1... | collective-permute-start | bytes 98312 | tf_op jit(solution)/shard_map/ppermute | solution.py:18
  208.8 5.2 %collective-permute-start.17 = (f32[64,128]{1,0:T(8,128)S(1)}, f32[64,128]{1,0:T(8,128)S(1)}, u32[]{:S(2)}, u32[]{:S(2)}) collective-permute-start(f32[64,128]{1,0:T(8,128)S(1)} %get-tuple-element.14), channel_id=1, source_target_pairs={{64,0},{128,64},{192,128},{256,192},{320,256},{384,320},{448,384},... | collective-permute-start | bytes 98312 | tf_op jit(solution)/shard_map/ppermute | solution.py:17
  227.4 29.9 %all-to-all-start.6 = ((f32[64,17,128]{2,1,0:T(8,128)}), f32[64,17,128]{2,1,0:T(8,128)S(1)}, u32[]{:S(2)}, u32[]{:S(2)}) async-start(f32[64,17,128]{2,1,0:T(8,128)} %broadcast_in_dim.63), calls=%async_computation.6 | async-start | bytes 1572864 | tf_op jit(solution)/shard_map/all_to_all | solution.py:37
  258.0 13.4 %collective-permute-start.20 = (f32[64,128]{1,0:T(8,128)S(1)}, f32[64,128]{1,0:T(8,128)S(1)}, u32[]{:S(2)}, u32[]{:S(2)}) collective-permute-start(f32[64,128]{1,0:T(8,128)S(1)} %get-tuple-element.7), channel_id=1, source_target_pairs={{0,64},{64,128},{128,192},{192,256},{256,320},{320,384},{384,448},... | collective-permute-start | bytes 98312 | tf_op jit(solution)/shard_map/ppermute | solution.py:16
  262.1 9.3 %collective-permute-start.23 = (f32[64,128]{1,0:T(8,128)S(1)}, f32[64,128]{1,0:T(8,128)S(1)}, u32[]{:S(2)}, u32[]{:S(2)}) collective-permute-start(f32[64,128]{1,0:T(8,128)S(1)} %get-tuple-element.8), channel_id=1, source_target_pairs={{1,0},{2,1},{3,2},{4,3},{5,4},{6,5},{7,6},{8,7},{9,8},{10,9},{11,1... | collective-permute-start | bytes 98312 | tf_op jit(solution)/shard_map/ppermute | solution.py:19
  264.2 7.2 %collective-permute-start.22 = (f32[64,128]{1,0:T(8,128)S(1)}, f32[64,128]{1,0:T(8,128)S(1)}, u32[]{:S(2)}, u32[]{:S(2)}) collective-permute-start(f32[64,128]{1,0:T(8,128)S(1)} %get-tuple-element.9), channel_id=1, source_target_pairs={{0,1},{1,2},{2,3},{3,4},{4,5},{5,6},{6,7},{7,8},{8,9},{9,10},{10,1... | collective-permute-start | bytes 98312 | tf_op jit(solution)/shard_map/ppermute | solution.py:18
  269.5 5.2 %collective-permute-start.21 = (f32[64,128]{1,0:T(8,128)S(1)}, f32[64,128]{1,0:T(8,128)S(1)}, u32[]{:S(2)}, u32[]{:S(2)}) collective-permute-start(f32[64,128]{1,0:T(8,128)S(1)} %get-tuple-element.10), channel_id=1, source_target_pairs={{64,0},{128,64},{192,128},{256,192},{320,256},{384,320},{448,384},... | collective-permute-start | bytes 98312 | tf_op jit(solution)/shard_map/ppermute | solution.py:17

commit v3 on v2

--- a/solution.py
+++ b/solution.py
@@ -8,16 +8,27 @@
 HIGHEST = lax.Precision.HIGHEST
 
 
+def pairs(axis, first):
+    peers = lax.axis_size(axis)
+    lower = range(first, peers - 1, 2)
+    return [(i, i + 1) for i in lower] + [(i + 1, i) for i in lower]
+
+
+def swap_across(low, high, axis):
+    even = lax.axis_index(axis) % 2 == 0
+    shifted = lax.ppermute(jnp.where(even, low, high), axis, pairs(axis, 1))
+    paired = lax.ppermute(jnp.where(even, high, low), axis, pairs(axis, 0))
+    return jnp.where(even, shifted, paired), jnp.where(even, paired, shifted)
+
+
+def partners(faces):
+    west, east = swap_across(faces[2], faces[3], "wide")
+    north, south = swap_across(faces[0], faces[1], "sub")
+    return jnp.stack([north, south, west, east])
+
+
 def assemble(faces):
-    rows = lax.axis_size("sub")
-    cols = lax.axis_size("wide")
-    down = [(i, i + 1) for i in range(rows - 1)]
-    right = [(i, i + 1) for i in range(cols - 1)]
-    from_north = lax.ppermute(faces[1], "sub", down)
-    from_south = lax.ppermute(faces[0], "sub", [(b, a) for a, b in down])
-    from_west = lax.ppermute(faces[3], "wide", right)
-    from_east = lax.ppermute(faces[2], "wide", [(b, a) for a, b in right])
-    return faces + jnp.stack([from_north, from_south, from_west, from_east])
+    return faces + partners(faces)
 
 
 def apply_local(faces, operator, selector_half, selector_full):
@@ -129,17 +140,25 @@
             inverse_rows = own_inverse_rows(corner_ids, ids, coarse_inverse)
             ids = ids.reshape(cols_total, 2, half_slots).transpose(1, 0, 2).reshape(-1)
             rows_at = pick_columns(inverse_rows, ids)
-            rows_at = rows_at.reshape(prims, 2, cols_total * half_slots)
-            rows_at = rows_at.transpose(1, 0, 2).reshape(2 * prims, -1)
+            sent = jnp.concatenate(
+                [jnp.broadcast_to(rows_at[None], (4, *rows_at.shape)), basis.transpose(1, 0, 2)], axis=2
+            )
+            sent = partners(sent)
+            partner_basis = sent[:, :, rows_at.shape[1] :]
+            rows_at = jnp.concatenate([rows_at[None], sent[:, :, : rows_at.shape[1]]])
+            rows_at = rows_at.reshape(5, prims, 2, cols_total * half_slots)
+            rows_at = rows_at.transpose(0, 2, 1, 3).reshape(10 * prims, -1)
         else:
             everyone = gather(summed, "wide")
         solved = jnp.dot(
             rows_at, everyone.reshape(cols_total * half_slots, 2 * rhs), precision=HIGHEST
         )
-        picked = solved[:prims, :rhs] + solved[prims:, rhs:]
+        solved = solved.reshape(5, 2, prims, 2 * rhs)
+        picked = solved[:, 0, :, :rhs] + solved[:, 1, :, rhs:]
         neumann_part = apply_local(weighted, neumann, selector_half, selector_full)
-        correction = jnp.einsum("pj,pfn->fjn", picked, basis, precision=HIGHEST)
-        update = assemble(weights * (neumann_part + correction))
+        correction = jnp.einsum("pj,pfn->fjn", picked[0], basis, precision=HIGHEST)
+        correction += jnp.einsum("fpj,fpn->fjn", picked[1:], partner_basis, precision=HIGHEST)
+        update = assemble(weights * neumann_part) + weights * correction
         solution = solution + damping * update
     return solution[None, None]
 

time: 277 us -> 241 us (0.87)
  waiting for transfers between devices: 96.5 us -> 63.5 us
  blocking collectives: 23.6 us -> 0 us
  starting transfers between devices: 129 us -> 143 us
    all_to_all x4 -> x6, waiting for transfers between devices: 71.4 us -> 35.9 us  [gather(): return lax.all_to_all(copies, axis, 0, 0, tiled=True)]
    all_to_all x2 -> x0, blocking collectives: 23.6 us -> none  [gather(): return lax.all_to_all(copies, axis, 0, 0, tiled=True)]
    all_to_all x4 -> x6, starting transfers between devices: 41.5 us -> 50.7 us  [gather(): return lax.all_to_all(copies, axis, 0, 0, tiled=True)]
    ppermute x24 -> x28, starting transfers between devices: 80.6 us -> 84 us  [the longest x14 51.7 us: swap_across(): shifted = lax.ppermute(jnp.where(even, low, high), axis, pairs(axis, 1))]
    ppermute x24 -> x28, waiting for transfers between devices: 16.5 us -> 18.9 us  [the longest x14 12.8 us: swap_across(): shifted = lax.ppermute(jnp.where(even, low, high), axis, pairs(axis, 1))]
  transfers between devices with their start and end apart: 29 -> 35, of which waited for: 11 -> 17; matrix products, arithmetic and copies ran while one was open for 2% -> 5% of each run, Pallas kernels for 0% -> 0%
where the time goes in v3:
time: 241 us; the launch traced here: 237 us
  starting transfers between devices  143 us (59%)
  waiting for transfers between devices  63.5 us (26%)
  matrix products  14.9 us (6%)
  local copies, waits for them, and re-layouts  9.9 us (4%)
  other arithmetic  4.47 us (2%)
    ppermute x14, starting transfers between devices, swap_across(): shifted = lax.ppermute(jnp.where(even, low, high), axis, pairs(axis, 1))  51.7 us
    all_to_all x6, starting transfers between devices, gather(): return lax.all_to_all(copies, axis, 0, 0, tiled=True)  50.7 us
    all_to_all x6, waiting for transfers between devices, gather(): return lax.all_to_all(copies, axis, 0, 0, tiled=True)  35.9 us
    ppermute x14, starting transfers between devices, swap_across(): paired = lax.ppermute(jnp.where(even, high, low), axis, pairs(axis, 0))  32.3 us
    ppermute x14, waiting for transfers between devices, swap_across(): shifted = lax.ppermute(jnp.where(even, low, high), axis, pairs(axis, 1))  12.8 us
    all_to_all x1, waiting for transfers between devices, own_inverse_rows(): lax.all_to_all(entries.reshape(peers, owned * slots), 'wide', 0, 0, tiled...  8.72 us
    all_to_all x1, starting transfers between devices, own_inverse_rows(): lax.all_to_all(entries.reshape(peers, owned * slots), 'wide', 0, 0, tiled...  8.2 us
    ppermute x14, waiting for transfers between devices, swap_across(): paired = lax.ppermute(jnp.where(even, high, low), axis, pairs(axis, 0))  6.1 us
  transfers between devices with their start and end apart: 35, of which 17 were waited for; matrix products, arithmetic and copies ran while one was open for 5% of the time, Pallas kernels for 0%

profile of v3, /device:TPU:15, one launch (start us, length us, event | category | flops | bytes accessed | tf_op | source)
XLA Modules:
  0.0 236.8 jit_solution(9538527362401774854)
XLA Ops:
  0.0 0.7 copy-done
  0.7 0.9 convolution_bitcast_fusion.3
  1.6 5.5 %collective-permute-start = (f32[64,128]{1,0:T(8,128)S(1)}, f32[64,128]{1,0:T(8,128)S(1)}, u32[]{:S(2)}, u32[]{:S(2)}) collective-permute-start(f32[64,128]{1,0:T(8,128)S(1)} %get-tuple-element.29), channel_id=1, source_target_pairs={{64,128},{192,256},{320,384},{448,512},{576,640},{704,768},{832,89... | collective-permute-start | bytes 98312 | tf_op jit(solution)/shard_map/ppermute | solution.py:19
  7.1 3.1 %collective-permute-start.2 = (f32[64,128]{1,0:T(8,128)S(1)}, f32[64,128]{1,0:T(8,128)S(1)}, u32[]{:S(2)}, u32[]{:S(2)}) collective-permute-start(f32[64,128]{1,0:T(8,128)S(1)} %get-tuple-element.30), channel_id=1, source_target_pairs={{1,2},{3,4},{5,6},{7,8},{9,10},{11,12},{13,14},{15,16},{17,18},{19... | collective-permute-start | bytes 98312 | tf_op jit(solution)/shard_map/ppermute | solution.py:19
  10.2 3.0 %collective-permute-start.3 = (f32[64,128]{1,0:T(8,128)S(1)}, f32[64,128]{1,0:T(8,128)S(1)}, u32[]{:S(2)}, u32[]{:S(2)}) collective-permute-start(f32[64,128]{1,0:T(8,128)S(1)} %get-tuple-element.31), channel_id=1, source_target_pairs={{0,1},{2,3},{4,5},{6,7},{8,9},{10,11},{12,13},{14,15},{16,17},{18,... | collective-permute-start | bytes 98312 | tf_op jit(solution)/shard_map/ppermute | solution.py:20
  13.2 1.9 collective-permute-start.1
  15.2 0.7 bitcast_convert_fusion
  15.8 0.9 reduce-precision_convert_fusion.1
  17.9 0.7 broadcast_in_dim.55
  18.5 15.4 %all-to-all-start = ((f32[16,4,128]{2,1,0:T(4,128)}), f32[16,4,128]{2,1,0:T(4,128)S(1)}, u32[]{:S(2)}, u32[]{:S(2)}) async-start(f32[16,4,128]{2,1,0:T(4,128)} %broadcast_in_dim.55), calls=%async_computation | async-start | bytes 65536 | tf_op jit(solution)/shard_map/all_to_all | solution.py:48
  34.2 7.1 %all-to-all-done = f32[16,4,128]{2,1,0:T(4,128)S(1)} async-done(((f32[16,4,128]{2,1,0:T(4,128)}), f32[16,4,128]{2,1,0:T(4,128)S(1)}, u32[]{:S(2)}, u32[]{:S(2)}) %all-to-all-start) | async-done | bytes 32800 | tf_op jit(solution)/shard_map/all_to_all | solution.py:48
  42.4 1.0 broadcast_in_dim.61
  43.3 11.2 %all-to-all-start.1 = ((f32[64,18,128]{2,1,0:T(8,128)}), f32[64,18,128]{2,1,0:T(8,128)S(1)}, u32[]{:S(2)}, u32[]{:S(2)}) async-start(f32[64,18,128]{2,1,0:T(8,128)} %broadcast_in_dim.61), calls=%async_computation.1 | async-start | bytes 1572864 | tf_op jit(solution)/shard_map/all_to_all | solution.py:48
  55.2 3.1 %collective-permute-start.6 = (f32[64,128]{1,0:T(8,128)S(1)}, f32[64,128]{1,0:T(8,128)S(1)}, u32[]{:S(2)}, u32[]{:S(2)}) collective-permute-start(f32[64,128]{1,0:T(8,128)S(1)} %get-tuple-element.26), channel_id=1, source_target_pairs={{1,2},{3,4},{5,6},{7,8},{9,10},{11,12},{13,14},{15,16},{17,18},{19... | collective-permute-start | bytes 98312 | tf_op jit(solution)/shard_map/ppermute | solution.py:19
  58.3 3.1 %collective-permute-start.7 = (f32[64,128]{1,0:T(8,128)S(1)}, f32[64,128]{1,0:T(8,128)S(1)}, u32[]{:S(2)}, u32[]{:S(2)}) collective-permute-start(f32[64,128]{1,0:T(8,128)S(1)} %get-tuple-element.27), channel_id=1, source_target_pairs={{0,1},{2,3},{4,5},{6,7},{8,9},{10,11},{12,13},{14,15},{16,17},{18,... | collective-permute-start | bytes 98312 | tf_op jit(solution)/shard_map/ppermute | solution.py:20
  61.7 3.6 %collective-permute-start.4 = (f32[64,128]{1,0:T(8,128)S(1)}, f32[64,128]{1,0:T(8,128)S(1)}, u32[]{:S(2)}, u32[]{:S(2)}) collective-permute-start(f32[64,128]{1,0:T(8,128)S(1)} %get-tuple-element.25), channel_id=1, source_target_pairs={{64,128},{192,256},{320,384},{448,512},{576,640},{704,768},{832,89... | collective-permute-start | bytes 98312 | tf_op jit(solution)/shard_map/ppermute | solution.py:19
  65.2 1.9 collective-permute-start.5
  67.1 3.7 %collective-permute-done.6 = f32[64,128]{1,0:T(8,128)S(1)} collective-permute-done((f32[64,128]{1,0:T(8,128)S(1)}, f32[64,128]{1,0:T(8,128)S(1)}, u32[]{:S(2)}, u32[]{:S(2)}) %collective-permute-start.6) | collective-permute-done | bytes 32800 | tf_op jit(solution)/shard_map/ppermute | solution.py:19
  70.8 1.2 collective-permute-done.7
  72.0 4.8 %all-to-all-done.1 = f32[64,18,128]{2,1,0:T(8,128)S(1)} async-done(((f32[64,18,128]{2,1,0:T(8,128)}), f32[64,18,128]{2,1,0:T(8,128)S(1)}, u32[]{:S(2)}, u32[]{:S(2)}) %all-to-all-start.1) | async-done | bytes 589856 | tf_op jit(solution)/shard_map/all_to_all | solution.py:48
  77.1 2.0 fusion
  79.2 0.7 reshape.205
  80.2 0.8 copy.137
  81.0 8.2 %all-to-all-start.2 = ((f32[64,1,612]{2,1,0:T(1,128)}), f32[64,1,612]{2,1,0:T(1,128)S(1)}, u32[]{:S(2)}, u32[]{:S(2)}) async-start(f32[64,1,612]{2,1,0:T(1,128)} %copy.137), calls=%async_computation.2 | async-start | bytes 327680 | tf_op jit(solution)/shard_map/all_to_all | solution.py:74
  89.7 8.7 %all-to-all-done.2 = f32[64,1,612]{2,1,0:T(1,128)S(1)} async-done(((f32[64,1,612]{2,1,0:T(1,128)}), f32[64,1,612]{2,1,0:T(1,128)S(1)}, u32[]{:S(2)}, u32[]{:S(2)}) %all-to-all-start.2) | async-done | bytes 156704 | tf_op jit(solution)/shard_map/all_to_all | solution.py:74
  99.6 1.8 fusion.1
  101.6 2.6 %collective-permute-start.11 = (f32[4,2304]{1,0:T(4,128)S(1)}, f32[4,2304]{1,0:T(4,128)S(1)}, u32[]{:S(2)}, u32[]{:S(2)}) collective-permute-start(f32[4,2304]{1,0:T(4,128)S(1)} %get-tuple-element.6), channel_id=1, source_target_pairs={{0,1},{2,3},{4,5},{6,7},{8,9},{10,11},{12,13},{14,15},{16,17},{18,... | collective-permute-start | bytes 110600 | tf_op jit(solution)/shard_map/ppermute | solution.py:20
  104.1 4.9 %collective-permute-start.10 = (f32[4,2304]{1,0:T(4,128)S(1)}, f32[4,2304]{1,0:T(4,128)S(1)}, u32[]{:S(2)}, u32[]{:S(2)}) collective-permute-start(f32[4,2304]{1,0:T(4,128)S(1)} %get-tuple-element.7), channel_id=1, source_target_pairs={{1,2},{3,4},{5,6},{7,8},{9,10},{11,12},{13,14},{15,16},{17,18},{19... | collective-permute-start | bytes 110600 | tf_op jit(solution)/shard_map/ppermute | solution.py:19
  109.2 5.0 %collective-permute-start.8 = (f32[4,2304]{1,0:T(4,128)S(1)}, f32[4,2304]{1,0:T(4,128)S(1)}, u32[]{:S(2)}, u32[]{:S(2)}) collective-permute-start(f32[4,2304]{1,0:T(4,128)S(1)} %get-tuple-element.5), channel_id=1, source_target_pairs={{64,128},{192,256},{320,384},{448,512},{576,640},{704,768},{832,89... | collective-permute-start | bytes 110600 | tf_op jit(solution)/shard_map/ppermute | solution.py:19
  114.3 2.1 collective-permute-start.9
  116.5 0.9 collective-permute-done.9
  120.1 2.4 %collective-permute-start.14 = (f32[64,128]{1,0:T(8,128)S(1)}, f32[64,128]{1,0:T(8,128)S(1)}, u32[]{:S(2)}, u32[]{:S(2)}) collective-permute-start(f32[64,128]{1,0:T(8,128)S(1)} %get-tuple-element.22), channel_id=1, source_target_pairs={{1,2},{3,4},{5,6},{7,8},{9,10},{11,12},{13,14},{15,16},{17,18},{19... | collective-permute-start | bytes 98312 | tf_op jit(solution)/shard_map/ppermute | solution.py:19
  122.5 1.9 collective-permute-start.15
  124.4 2.6 %collective-permute-start.12 = (f32[64,128]{1,0:T(8,128)S(1)}, f32[64,128]{1,0:T(8,128)S(1)}, u32[]{:S(2)}, u32[]{:S(2)}) collective-permute-start(f32[64,128]{1,0:T(8,128)S(1)} %get-tuple-element.21), channel_id=1, source_target_pairs={{64,128},{192,256},{320,384},{448,512},{576,640},{704,768},{832,89... | collective-permute-start | bytes 98312 | tf_op jit(solution)/shard_map/ppermute | solution.py:19
  127.0 1.9 collective-permute-start.13
  129.0 0.6 collective-permute-done.12
  131.5 4.4 %all-to-all-start.3 = ((f32[16,4,128]{2,1,0:T(4,128)}), f32[16,4,128]{2,1,0:T(4,128)S(1)}, u32[]{:S(2)}, u32[]{:S(2)}) async-start(f32[16,4,128]{2,1,0:T(4,128)} %broadcast_in_dim.63), calls=%async_computation.3 | async-start | bytes 65536 | tf_op jit(solution)/shard_map/all_to_all | solution.py:48
  136.1 7.1 %all-to-all-done.3 = f32[16,4,128]{2,1,0:T(4,128)S(1)} async-done(((f32[16,4,128]{2,1,0:T(4,128)}), f32[16,4,128]{2,1,0:T(4,128)S(1)}, u32[]{:S(2)}, u32[]{:S(2)}) %all-to-all-start.3) | async-done | bytes 32800 | tf_op jit(solution)/shard_map/all_to_all | solution.py:48
  143.5 1.0 broadcast_in_dim.64
  144.5 8.3 %all-to-all-start.4 = ((f32[64,17,128]{2,1,0:T(8,128)}), f32[64,17,128]{2,1,0:T(8,128)S(1)}, u32[]{:S(2)}, u32[]{:S(2)}) async-start(f32[64,17,128]{2,1,0:T(8,128)} %broadcast_in_dim.64), calls=%async_computation.4 | async-start | bytes 1572864 | tf_op jit(solution)/shard_map/all_to_all | solution.py:48
  153.2 3.1 %collective-permute-start.18 = (f32[64,128]{1,0:T(8,128)S(1)}, f32[64,128]{1,0:T(8,128)S(1)}, u32[]{:S(2)}, u32[]{:S(2)}) collective-permute-start(f32[64,128]{1,0:T(8,128)S(1)} %get-tuple-element.18), channel_id=1, source_target_pairs={{1,2},{3,4},{5,6},{7,8},{9,10},{11,12},{13,14},{15,16},{17,18},{19... | collective-permute-start | bytes 98312 | tf_op jit(solution)/shard_map/ppermute | solution.py:19
  156.3 3.1 %collective-permute-start.19 = (f32[64,128]{1,0:T(8,128)S(1)}, f32[64,128]{1,0:T(8,128)S(1)}, u32[]{:S(2)}, u32[]{:S(2)}) collective-permute-start(f32[64,128]{1,0:T(8,128)S(1)} %get-tuple-element.19), channel_id=1, source_target_pairs={{0,1},{2,3},{4,5},{6,7},{8,9},{10,11},{12,13},{14,15},{16,17},{18,... | collective-permute-start | bytes 98312 | tf_op jit(solution)/shard_map/ppermute | solution.py:20
  159.4 3.6 %collective-permute-start.16 = (f32[64,128]{1,0:T(8,128)S(1)}, f32[64,128]{1,0:T(8,128)S(1)}, u32[]{:S(2)}, u32[]{:S(2)}) collective-permute-start(f32[64,128]{1,0:T(8,128)S(1)} %get-tuple-element.17), channel_id=1, source_target_pairs={{64,128},{192,256},{320,384},{448,512},{576,640},{704,768},{832,89... | collective-permute-start | bytes 98312 | tf_op jit(solution)/shard_map/ppermute | solution.py:19
  162.9 1.9 collective-permute-start.17
  164.9 4.2 %collective-permute-done.18 = f32[64,128]{1,0:T(8,128)S(1)} collective-permute-done((f32[64,128]{1,0:T(8,128)S(1)}, f32[64,128]{1,0:T(8,128)S(1)}, u32[]{:S(2)}, u32[]{:S(2)}) %collective-permute-start.18) | collective-permute-done | bytes 32800 | tf_op jit(solution)/shard_map/ppermute | solution.py:19
  169.1 1.2 collective-permute-done.19
  170.3 4.8 %all-to-all-done.4 = f32[64,17,128]{2,1,0:T(8,128)S(1)} async-done(((f32[64,17,128]{2,1,0:T(8,128)}), f32[64,17,128]{2,1,0:T(8,128)S(1)}, u32[]{:S(2)}, u32[]{:S(2)}) %all-to-all-start.4) | async-done | bytes 557088 | tf_op jit(solution)/shard_map/all_to_all | solution.py:48
  177.5 3.3 %collective-permute-start.22 = (f32[64,128]{1,0:T(8,128)S(1)}, f32[64,128]{1,0:T(8,128)S(1)}, u32[]{:S(2)}, u32[]{:S(2)}) collective-permute-start(f32[64,128]{1,0:T(8,128)S(1)} %get-tuple-element.14), channel_id=1, source_target_pairs={{1,2},{3,4},{5,6},{7,8},{9,10},{11,12},{13,14},{15,16},{17,18},{19... | collective-permute-start | bytes 98312 | tf_op jit(solution)/shard_map/ppermute | solution.py:19
  180.8 1.9 collective-permute-start.23
  182.8 4.9 %collective-permute-start.20 = (f32[64,128]{1,0:T(8,128)S(1)}, f32[64,128]{1,0:T(8,128)S(1)}, u32[]{:S(2)}, u32[]{:S(2)}) collective-permute-start(f32[64,128]{1,0:T(8,128)S(1)} %get-tuple-element.13), channel_id=1, source_target_pairs={{64,128},{192,256},{320,384},{448,512},{576,640},{704,768},{832,89... | collective-permute-start | bytes 98312 | tf_op jit(solution)/shard_map/ppermute | solution.py:19
  187.7 1.9 collective-permute-start.21
  189.7 1.1 collective-permute-done.21
  192.1 3.4 %all-to-all-start.5 = ((f32[16,4,128]{2,1,0:T(4,128)}), f32[16,4,128]{2,1,0:T(4,128)S(1)}, u32[]{:S(2)}, u32[]{:S(2)}) async-start(f32[16,4,128]{2,1,0:T(4,128)} %broadcast_in_dim.65), calls=%async_computation.5 | async-start | bytes 65536 | tf_op jit(solution)/shard_map/all_to_all | solution.py:48
  195.9 7.2 %all-to-all-done.5 = f32[16,4,128]{2,1,0:T(4,128)S(1)} async-done(((f32[16,4,128]{2,1,0:T(4,128)}), f32[16,4,128]{2,1,0:T(4,128)S(1)}, u32[]{:S(2)}, u32[]{:S(2)}) %all-to-all-start.5) | async-done | bytes 32800 | tf_op jit(solution)/shard_map/all_to_all | solution.py:48
  203.3 1.0 broadcast_in_dim.66
  204.3 8.1 %all-to-all-start.6 = ((f32[64,17,128]{2,1,0:T(8,128)}), f32[64,17,128]{2,1,0:T(8,128)S(1)}, u32[]{:S(2)}, u32[]{:S(2)}) async-start(f32[64,17,128]{2,1,0:T(8,128)} %broadcast_in_dim.66), calls=%async_computation.6 | async-start | bytes 1572864 | tf_op jit(solution)/shard_map/all_to_all | solution.py:48
  212.8 3.1 %collective-permute-start.26 = (f32[64,128]{1,0:T(8,128)S(1)}, f32[64,128]{1,0:T(8,128)S(1)}, u32[]{:S(2)}, u32[]{:S(2)}) collective-permute-start(f32[64,128]{1,0:T(8,128)S(1)} %get-tuple-element.10), channel_id=1, source_target_pairs={{1,2},{3,4},{5,6},{7,8},{9,10},{11,12},{13,14},{15,16},{17,18},{19... | collective-permute-start | bytes 98312 | tf_op jit(solution)/shard_map/ppermute | solution.py:19
  215.9 3.1 %collective-permute-start.27 = (f32[64,128]{1,0:T(8,128)S(1)}, f32[64,128]{1,0:T(8,128)S(1)}, u32[]{:S(2)}, u32[]{:S(2)}) collective-permute-start(f32[64,128]{1,0:T(8,128)S(1)} %get-tuple-element.11), channel_id=1, source_target_pairs={{0,1},{2,3},{4,5},{6,7},{8,9},{10,11},{12,13},{14,15},{16,17},{18,... | collective-permute-start | bytes 98312 | tf_op jit(solution)/shard_map/ppermute | solution.py:20
  219.0 3.5 %collective-permute-start.24 = (f32[64,128]{1,0:T(8,128)S(1)}, f32[64,128]{1,0:T(8,128)S(1)}, u32[]{:S(2)}, u32[]{:S(2)}) collective-permute-start(f32[64,128]{1,0:T(8,128)S(1)} %get-tuple-element.9), channel_id=1, source_target_pairs={{64,128},{192,256},{320,384},{448,512},{576,640},{704,768},{832,89... | collective-permute-start | bytes 98312 | tf_op jit(solution)/shard_map/ppermute | solution.py:19
  222.5 1.9 collective-permute-start.25
  224.4 4.2 %collective-permute-done.26 = f32[64,128]{1,0:T(8,128)S(1)} collective-permute-done((f32[64,128]{1,0:T(8,128)S(1)}, f32[64,128]{1,0:T(8,128)S(1)}, u32[]{:S(2)}, u32[]{:S(2)}) %collective-permute-start.26) | collective-permute-done | bytes 32800 | tf_op jit(solution)/shard_map/ppermute | solution.py:19
  228.7 1.2 collective-permute-done.27
  229.9 4.8 %all-to-all-done.6 = f32[64,17,128]{2,1,0:T(8,128)S(1)} async-done(((f32[64,17,128]{2,1,0:T(8,128)}), f32[64,17,128]{2,1,0:T(8,128)S(1)}, u32[]{:S(2)}, u32[]{:S(2)}) %all-to-all-start.6) | async-done | bytes 557088 | tf_op jit(solution)/shard_map/all_to_all | solution.py:48
  235.8 1.1 fusion.29
  (151 shorter events, 16.7 us)
Async XLA Ops:
  0.0 0.7 copy-start
  0.0 16.8 %copy-start.1 = (bf16[1,1,512,512]{3,2,1,0:T(8,128)(2,1)S(1)}, bf16[1,1,512,512]{3,2,1,0:T(8,128)(2,1)}, u32[]{:S(2)}) copy-start(bf16[1,1,512,512]{3,2,1,0:T(8,128)(2,1)} %param.12) | copy-start | bytes 1572868
  1.6 15.5 %collective-permute-start = (f32[64,128]{1,0:T(8,128)S(1)}, f32[64,128]{1,0:T(8,128)S(1)}, u32[]{:S(2)}, u32[]{:S(2)}) collective-permute-start(f32[64,128]{1,0:T(8,128)S(1)} %get-tuple-element.29), channel_id=1, source_target_pairs={{64,128},{192,256},{320,384},{448,512},{576,640},{704,768},{832,89... | collective-permute-start | bytes 98312 | tf_op jit(solution)/shard_map/ppermute | solution.py:19
  7.1 10.0 %collective-permute-start.2 = (f32[64,128]{1,0:T(8,128)S(1)}, f32[64,128]{1,0:T(8,128)S(1)}, u32[]{:S(2)}, u32[]{:S(2)}) collective-permute-start(f32[64,128]{1,0:T(8,128)S(1)} %get-tuple-element.30), channel_id=1, source_target_pairs={{1,2},{3,4},{5,6},{7,8},{9,10},{11,12},{13,14},{15,16},{17,18},{19... | collective-permute-start | bytes 98312 | tf_op jit(solution)/shard_map/ppermute | solution.py:19
  10.2 6.9 %collective-permute-start.3 = (f32[64,128]{1,0:T(8,128)S(1)}, f32[64,128]{1,0:T(8,128)S(1)}, u32[]{:S(2)}, u32[]{:S(2)}) collective-permute-start(f32[64,128]{1,0:T(8,128)S(1)} %get-tuple-element.31), channel_id=1, source_target_pairs={{0,1},{2,3},{4,5},{6,7},{8,9},{10,11},{12,13},{14,15},{16,17},{18,... | collective-permute-start | bytes 98312 | tf_op jit(solution)/shard_map/ppermute | solution.py:20
  13.2 3.9 %collective-permute-start.1 = (f32[64,128]{1,0:T(8,128)S(1)}, f32[64,128]{1,0:T(8,128)S(1)}, u32[]{:S(2)}, u32[]{:S(2)}) collective-permute-start(f32[64,128]{1,0:T(8,128)S(1)} %get-tuple-element.32), channel_id=1, source_target_pairs={{0,64},{128,192},{256,320},{384,448},{512,576},{640,704},{768,832}... | collective-permute-start | bytes 98312 | tf_op jit(solution)/shard_map/ppermute | solution.py:20
  16.8 0.7 copy-start.3
  16.8 17.1 %copy-start.4 = (s32[1,1,4]{2,1,0:T(1,128)S(1)}, s32[1,1,4]{2,1,0:T(1,128)}, u32[]{:S(2)}) copy-start(s32[1,1,4]{2,1,0:T(1,128)} %param.10) | copy-start | bytes 52
  18.5 22.8 %all-to-all-start = ((f32[16,4,128]{2,1,0:T(4,128)}), f32[16,4,128]{2,1,0:T(4,128)S(1)}, u32[]{:S(2)}, u32[]{:S(2)}) async-start(f32[16,4,128]{2,1,0:T(4,128)} %broadcast_in_dim.55), calls=%async_computation | async-start | bytes 65536 | tf_op jit(solution)/shard_map/all_to_all | solution.py:48
  43.3 33.5 %all-to-all-start.1 = ((f32[64,18,128]{2,1,0:T(8,128)}), f32[64,18,128]{2,1,0:T(8,128)S(1)}, u32[]{:S(2)}, u32[]{:S(2)}) async-start(f32[64,18,128]{2,1,0:T(8,128)} %broadcast_in_dim.61), calls=%async_computation.1 | async-start | bytes 1572864 | tf_op jit(solution)/shard_map/all_to_all | solution.py:48
  54.5 6.9 %copy-start.2 = (bf16[1,1,512,512]{3,2,1,0:T(8,128)(2,1)S(1)}, bf16[1,1,512,512]{3,2,1,0:T(8,128)(2,1)}, u32[]{:S(2)}) copy-start(bf16[1,1,512,512]{3,2,1,0:T(8,128)(2,1)} %param.11) | copy-start | bytes 1572868
  55.2 15.6 %collective-permute-start.6 = (f32[64,128]{1,0:T(8,128)S(1)}, f32[64,128]{1,0:T(8,128)S(1)}, u32[]{:S(2)}, u32[]{:S(2)}) collective-permute-start(f32[64,128]{1,0:T(8,128)S(1)} %get-tuple-element.26), channel_id=1, source_target_pairs={{1,2},{3,4},{5,6},{7,8},{9,10},{11,12},{13,14},{15,16},{17,18},{19... | collective-permute-start | bytes 98312 | tf_op jit(solution)/shard_map/ppermute | solution.py:19
  58.3 13.7 %collective-permute-start.7 = (f32[64,128]{1,0:T(8,128)S(1)}, f32[64,128]{1,0:T(8,128)S(1)}, u32[]{:S(2)}, u32[]{:S(2)}) collective-permute-start(f32[64,128]{1,0:T(8,128)S(1)} %get-tuple-element.27), channel_id=1, source_target_pairs={{0,1},{2,3},{4,5},{6,7},{8,9},{10,11},{12,13},{14,15},{16,17},{18,... | collective-permute-start | bytes 98312 | tf_op jit(solution)/shard_map/ppermute | solution.py:20
  61.7 47.3 %collective-permute-start.4 = (f32[64,128]{1,0:T(8,128)S(1)}, f32[64,128]{1,0:T(8,128)S(1)}, u32[]{:S(2)}, u32[]{:S(2)}) collective-permute-start(f32[64,128]{1,0:T(8,128)S(1)} %get-tuple-element.25), channel_id=1, source_target_pairs={{64,128},{192,256},{320,384},{448,512},{576,640},{704,768},{832,89... | collective-permute-start | bytes 98312 | tf_op jit(solution)/shard_map/ppermute | solution.py:19
  65.2 43.8 %collective-permute-start.5 = (f32[64,128]{1,0:T(8,128)S(1)}, f32[64,128]{1,0:T(8,128)S(1)}, u32[]{:S(2)}, u32[]{:S(2)}) collective-permute-start(f32[64,128]{1,0:T(8,128)S(1)} %get-tuple-element.28), channel_id=1, source_target_pairs={{0,64},{128,192},{256,320},{384,448},{512,576},{640,704},{768,832}... | collective-permute-start | bytes 98312 | tf_op jit(solution)/shard_map/ppermute | solution.py:20
  81.0 17.4 %all-to-all-start.2 = ((f32[64,1,612]{2,1,0:T(1,128)}), f32[64,1,612]{2,1,0:T(1,128)S(1)}, u32[]{:S(2)}, u32[]{:S(2)}) async-start(f32[64,1,612]{2,1,0:T(1,128)} %copy.137), calls=%async_computation.2 | async-start | bytes 327680 | tf_op jit(solution)/shard_map/all_to_all | solution.py:74
  89.2 10.0 %copy-start.5 = (s32[1,1,4]{2,1,0:T(1,128)S(1)}, s32[1,1,4]{2,1,0:T(1,128)}, u32[]{:S(2)}) copy-start(s32[1,1,4]{2,1,0:T(1,128)} %param.14) | copy-start | bytes 52
  101.6 14.9 %collective-permute-start.11 = (f32[4,2304]{1,0:T(4,128)S(1)}, f32[4,2304]{1,0:T(4,128)S(1)}, u32[]{:S(2)}, u32[]{:S(2)}) collective-permute-start(f32[4,2304]{1,0:T(4,128)S(1)} %get-tuple-element.6), channel_id=1, source_target_pairs={{0,1},{2,3},{4,5},{6,7},{8,9},{10,11},{12,13},{14,15},{16,17},{18,... | collective-permute-start | bytes 110600 | tf_op jit(solution)/shard_map/ppermute | solution.py:20
  104.1 12.3 %collective-permute-start.10 = (f32[4,2304]{1,0:T(4,128)S(1)}, f32[4,2304]{1,0:T(4,128)S(1)}, u32[]{:S(2)}, u32[]{:S(2)}) collective-permute-start(f32[4,2304]{1,0:T(4,128)S(1)} %get-tuple-element.7), channel_id=1, source_target_pairs={{1,2},{3,4},{5,6},{7,8},{9,10},{11,12},{13,14},{15,16},{17,18},{19... | collective-permute-start | bytes 110600 | tf_op jit(solution)/shard_map/ppermute | solution.py:19
  109.2 7.2 %collective-permute-start.8 = (f32[4,2304]{1,0:T(4,128)S(1)}, f32[4,2304]{1,0:T(4,128)S(1)}, u32[]{:S(2)}, u32[]{:S(2)}) collective-permute-start(f32[4,2304]{1,0:T(4,128)S(1)} %get-tuple-element.5), channel_id=1, source_target_pairs={{64,128},{192,256},{320,384},{448,512},{576,640},{704,768},{832,89... | collective-permute-start | bytes 110600 | tf_op jit(solution)/shard_map/ppermute | solution.py:19
  114.3 3.1 %collective-permute-start.9 = (f32[4,2304]{1,0:T(4,128)S(1)}, f32[4,2304]{1,0:T(4,128)S(1)}, u32[]{:S(2)}, u32[]{:S(2)}) collective-permute-start(f32[4,2304]{1,0:T(4,128)S(1)} %get-tuple-element.8), channel_id=1, source_target_pairs={{0,64},{128,192},{256,320},{384,448},{512,576},{640,704},{768,832}... | collective-permute-start | bytes 110600 | tf_op jit(solution)/shard_map/ppermute | solution.py:20
  120.1 8.9 %collective-permute-start.14 = (f32[64,128]{1,0:T(8,128)S(1)}, f32[64,128]{1,0:T(8,128)S(1)}, u32[]{:S(2)}, u32[]{:S(2)}) collective-permute-start(f32[64,128]{1,0:T(8,128)S(1)} %get-tuple-element.22), channel_id=1, source_target_pairs={{1,2},{3,4},{5,6},{7,8},{9,10},{11,12},{13,14},{15,16},{17,18},{19... | collective-permute-start | bytes 98312 | tf_op jit(solution)/shard_map/ppermute | solution.py:19
  122.5 6.5 %collective-permute-start.15 = (f32[64,128]{1,0:T(8,128)S(1)}, f32[64,128]{1,0:T(8,128)S(1)}, u32[]{:S(2)}, u32[]{:S(2)}) collective-permute-start(f32[64,128]{1,0:T(8,128)S(1)} %get-tuple-element.23), channel_id=1, source_target_pairs={{0,1},{2,3},{4,5},{6,7},{8,9},{10,11},{12,13},{14,15},{16,17},{18,... | collective-permute-start | bytes 98312 | tf_op jit(solution)/shard_map/ppermute | solution.py:20
  124.4 5.2 %collective-permute-start.12 = (f32[64,128]{1,0:T(8,128)S(1)}, f32[64,128]{1,0:T(8,128)S(1)}, u32[]{:S(2)}, u32[]{:S(2)}) collective-permute-start(f32[64,128]{1,0:T(8,128)S(1)} %get-tuple-element.21), channel_id=1, source_target_pairs={{64,128},{192,256},{320,384},{448,512},{576,640},{704,768},{832,89... | collective-permute-start | bytes 98312 | tf_op jit(solution)/shard_map/ppermute | solution.py:19
  127.0 3.1 %collective-permute-start.13 = (f32[64,128]{1,0:T(8,128)S(1)}, f32[64,128]{1,0:T(8,128)S(1)}, u32[]{:S(2)}, u32[]{:S(2)}) collective-permute-start(f32[64,128]{1,0:T(8,128)S(1)} %get-tuple-element.24), channel_id=1, source_target_pairs={{0,64},{128,192},{256,320},{384,448},{512,576},{640,704},{768,832}... | collective-permute-start | bytes 98312 | tf_op jit(solution)/shard_map/ppermute | solution.py:20
  131.5 11.8 %all-to-all-start.3 = ((f32[16,4,128]{2,1,0:T(4,128)}), f32[16,4,128]{2,1,0:T(4,128)S(1)}, u32[]{:S(2)}, u32[]{:S(2)}) async-start(f32[16,4,128]{2,1,0:T(4,128)} %broadcast_in_dim.63), calls=%async_computation.3 | async-start | bytes 65536 | tf_op jit(solution)/shard_map/all_to_all | solution.py:48
  144.5 30.6 %all-to-all-start.4 = ((f32[64,17,128]{2,1,0:T(8,128)}), f32[64,17,128]{2,1,0:T(8,128)S(1)}, u32[]{:S(2)}, u32[]{:S(2)}) async-start(f32[64,17,128]{2,1,0:T(8,128)} %broadcast_in_dim.64), calls=%async_computation.4 | async-start | bytes 1572864 | tf_op jit(solution)/shard_map/all_to_all | solution.py:48
  153.2 15.9 %collective-permute-start.18 = (f32[64,128]{1,0:T(8,128)S(1)}, f32[64,128]{1,0:T(8,128)S(1)}, u32[]{:S(2)}, u32[]{:S(2)}) collective-permute-start(f32[64,128]{1,0:T(8,128)S(1)} %get-tuple-element.18), channel_id=1, source_target_pairs={{1,2},{3,4},{5,6},{7,8},{9,10},{11,12},{13,14},{15,16},{17,18},{19... | collective-permute-start | bytes 98312 | tf_op jit(solution)/shard_map/ppermute | solution.py:19
  156.3 14.0 %collective-permute-start.19 = (f32[64,128]{1,0:T(8,128)S(1)}, f32[64,128]{1,0:T(8,128)S(1)}, u32[]{:S(2)}, u32[]{:S(2)}) collective-permute-start(f32[64,128]{1,0:T(8,128)S(1)} %get-tuple-element.19), channel_id=1, source_target_pairs={{0,1},{2,3},{4,5},{6,7},{8,9},{10,11},{12,13},{14,15},{16,17},{18,... | collective-permute-start | bytes 98312 | tf_op jit(solution)/shard_map/ppermute | solution.py:20
  159.4 10.9 %collective-permute-start.16 = (f32[64,128]{1,0:T(8,128)S(1)}, f32[64,128]{1,0:T(8,128)S(1)}, u32[]{:S(2)}, u32[]{:S(2)}) collective-permute-start(f32[64,128]{1,0:T(8,128)S(1)} %get-tuple-element.17), channel_id=1, source_target_pairs={{64,128},{192,256},{320,384},{448,512},{576,640},{704,768},{832,89... | collective-permute-start | bytes 98312 | tf_op jit(solution)/shard_map/ppermute | solution.py:19
  162.9 7.3 %collective-permute-start.17 = (f32[64,128]{1,0:T(8,128)S(1)}, f32[64,128]{1,0:T(8,128)S(1)}, u32[]{:S(2)}, u32[]{:S(2)}) collective-permute-start(f32[64,128]{1,0:T(8,128)S(1)} %get-tuple-element.20), channel_id=1, source_target_pairs={{0,64},{128,192},{256,320},{384,448},{512,576},{640,704},{768,832}... | collective-permute-start | bytes 98312 | tf_op jit(solution)/shard_map/ppermute | solution.py:20
  177.5 12.1 %collective-permute-start.22 = (f32[64,128]{1,0:T(8,128)S(1)}, f32[64,128]{1,0:T(8,128)S(1)}, u32[]{:S(2)}, u32[]{:S(2)}) collective-permute-start(f32[64,128]{1,0:T(8,128)S(1)} %get-tuple-element.14), channel_id=1, source_target_pairs={{1,2},{3,4},{5,6},{7,8},{9,10},{11,12},{13,14},{15,16},{17,18},{19... | collective-permute-start | bytes 98312 | tf_op jit(solution)/shard_map/ppermute | solution.py:19
  180.8 8.8 %collective-permute-start.23 = (f32[64,128]{1,0:T(8,128)S(1)}, f32[64,128]{1,0:T(8,128)S(1)}, u32[]{:S(2)}, u32[]{:S(2)}) collective-permute-start(f32[64,128]{1,0:T(8,128)S(1)} %get-tuple-element.15), channel_id=1, source_target_pairs={{0,1},{2,3},{4,5},{6,7},{8,9},{10,11},{12,13},{14,15},{16,17},{18,... | collective-permute-start | bytes 98312 | tf_op jit(solution)/shard_map/ppermute | solution.py:20
  182.8 6.9 %collective-permute-start.20 = (f32[64,128]{1,0:T(8,128)S(1)}, f32[64,128]{1,0:T(8,128)S(1)}, u32[]{:S(2)}, u32[]{:S(2)}) collective-permute-start(f32[64,128]{1,0:T(8,128)S(1)} %get-tuple-element.13), channel_id=1, source_target_pairs={{64,128},{192,256},{320,384},{448,512},{576,640},{704,768},{832,89... | collective-permute-start | bytes 98312 | tf_op jit(solution)/shard_map/ppermute | solution.py:19
  187.7 3.1 %collective-permute-start.21 = (f32[64,128]{1,0:T(8,128)S(1)}, f32[64,128]{1,0:T(8,128)S(1)}, u32[]{:S(2)}, u32[]{:S(2)}) collective-permute-start(f32[64,128]{1,0:T(8,128)S(1)} %get-tuple-element.16), channel_id=1, source_target_pairs={{0,64},{128,192},{256,320},{384,448},{512,576},{640,704},{768,832}... | collective-permute-start | bytes 98312 | tf_op jit(solution)/shard_map/ppermute | solution.py:20
  192.1 10.9 %all-to-all-start.5 = ((f32[16,4,128]{2,1,0:T(4,128)}), f32[16,4,128]{2,1,0:T(4,128)S(1)}, u32[]{:S(2)}, u32[]{:S(2)}) async-start(f32[16,4,128]{2,1,0:T(4,128)} %broadcast_in_dim.65), calls=%async_computation.5 | async-start | bytes 65536 | tf_op jit(solution)/shard_map/all_to_all | solution.py:48
  204.3 30.5 %all-to-all-start.6 = ((f32[64,17,128]{2,1,0:T(8,128)}), f32[64,17,128]{2,1,0:T(8,128)S(1)}, u32[]{:S(2)}, u32[]{:S(2)}) async-start(f32[64,17,128]{2,1,0:T(8,128)} %broadcast_in_dim.66), calls=%async_computation.6 | async-start | bytes 1572864 | tf_op jit(solution)/shard_map/all_to_all | solution.py:48
  212.8 15.9 %collective-permute-start.26 = (f32[64,128]{1,0:T(8,128)S(1)}, f32[64,128]{1,0:T(8,128)S(1)}, u32[]{:S(2)}, u32[]{:S(2)}) collective-permute-start(f32[64,128]{1,0:T(8,128)S(1)} %get-tuple-element.10), channel_id=1, source_target_pairs={{1,2},{3,4},{5,6},{7,8},{9,10},{11,12},{13,14},{15,16},{17,18},{19... | collective-permute-start | bytes 98312 | tf_op jit(solution)/shard_map/ppermute | solution.py:19
  215.9 14.0 %collective-permute-start.27 = (f32[64,128]{1,0:T(8,128)S(1)}, f32[64,128]{1,0:T(8,128)S(1)}, u32[]{:S(2)}, u32[]{:S(2)}) collective-permute-start(f32[64,128]{1,0:T(8,128)S(1)} %get-tuple-element.11), channel_id=1, source_target_pairs={{0,1},{2,3},{4,5},{6,7},{8,9},{10,11},{12,13},{14,15},{16,17},{18,... | collective-permute-start | bytes 98312 | tf_op jit(solution)/shard_map/ppermute | solution.py:20
  219.0 10.9 %collective-permute-start.24 = (f32[64,128]{1,0:T(8,128)S(1)}, f32[64,128]{1,0:T(8,128)S(1)}, u32[]{:S(2)}, u32[]{:S(2)}) collective-permute-start(f32[64,128]{1,0:T(8,128)S(1)} %get-tuple-element.9), channel_id=1, source_target_pairs={{64,128},{192,256},{320,384},{448,512},{576,640},{704,768},{832,89... | collective-permute-start | bytes 98312 | tf_op jit(solution)/shard_map/ppermute | solution.py:19
  222.5 7.4 %collective-permute-start.25 = (f32[64,128]{1,0:T(8,128)S(1)}, f32[64,128]{1,0:T(8,128)S(1)}, u32[]{:S(2)}, u32[]{:S(2)}) collective-permute-start(f32[64,128]{1,0:T(8,128)S(1)} %get-tuple-element.12), channel_id=1, source_target_pairs={{0,64},{128,192},{256,320},{384,448},{512,576},{640,704},{768,832}... | collective-permute-start | bytes 98312 | tf_op jit(solution)/shard_map/ppermute | solution.py:20
